TPU v7x, 128 devices: a whole 4x4x4 slice. The times are simulated.
128 devices in a mesh: tri: 2 (over x_hi), blk: 64 (over y, x_lo, z, core).
Axes of the slice: x: 4 (x_hi: 2, x_lo: 2; x = x_hi * 2 + x_lo), y: 4, z: 4, core: 2. Of those that a mesh axis runs over, the one named last changes fastest.
Arguments:
- layers: float32 [384, 4, 393216], P(('tri', 'blk')), as said below
- tile_mask: int32 [384, 1, 24], P(('tri', 'blk')), may hold values 0 or 1
- depth_order: int32 [384], replicated, may hold values from 0 to 383, as said below
Outputs:
- composite: float32 [4, 393216], P(None, 'blk')
Inputs may be any that keep to these rules, and one draw needn't show every extreme that they name: `layers`: in each rank's layer the first three channels lie between 0 and channel 3, and channel 3 lies between 0 and 6 / 384. `depth_order`: A permutation. Ranks are numbered so that device d of the mesh (tri index times 64 plus blk index) holds ranks 3 * d to 3 * d + 2, and these take consecutive positions. The 64 devices of one tri index hold consecutive positions, and for every bit b, the devices of one tri index that agree on all bits of the blk index above bit b hold consecutive positions.
All inputs are finite; a program needn't handle non-finite values. No bound on the sum of `tile_mask` on one device may be relied on, other than what follows from the above.
Results may differ from a plain program's by a relative error of at most 0.00002.
Values sent between devices are 32-bit elements; how exact they have to be, the bound alone decides.
A program may use at most 128 MiB of HBM per device.

v0:
```python
import jax
import jax.numpy as jnp
from jax import lax
from jax.sharding import PartitionSpec as P

WIDTH = 3072
TILE = 128


def blend_pair(nearer, farther):
    return nearer + (1.0 - nearer[3:4]) * farther


def blend_ordered(ordered):
    while ordered.shape[1] > 1:
        paired = ordered.reshape(4, ordered.shape[1] // 2, 2, ordered.shape[2])
        ordered = blend_pair(paired[:, :, 0], paired[:, :, 1])
    return ordered[:, 0]


def blend_group(stacked, depths):
    members = stacked.shape[1]
    summed = jnp.zeros_like(stacked[:, 0])
    for source in range(members):
        through = jnp.ones_like(stacked[3, 0])
        for other in range(members):
            if other != source:
                through = through * jnp.where(
                    depths[other] < depths[source], 1.0 - stacked[3, other], 1.0
                )
        summed = summed + through[None] * stacked[:, source]
    return summed


def on_device(layers, tile_mask, depth_order):
    blk_count = lax.axis_size("blk")
    tri_count = lax.axis_size("tri")
    blk_index = lax.axis_index("blk")
    tri_index = lax.axis_index("tri")
    device_index = tri_index * blk_count + blk_index
    rank_dev = layers.shape[0]
    pixels = layers.shape[2]
    tile_rows = pixels // WIDTH // TILE
    tile_on = tile_mask.astype(jnp.float32)
    masked = (
        layers.reshape(rank_dev, 4, tile_rows, TILE, WIDTH // TILE, TILE)
        * tile_on[:, None, :, None, :, None]
    )
    masked = masked.reshape(rank_dev, 4, pixels)
    own_depths = lax.dynamic_slice_in_dim(depth_order, device_index * rank_dev, rank_dev)
    local_image = blend_group(jnp.moveaxis(masked, 0, 1), own_depths)
    device_depth = jnp.min(depth_order.reshape(-1, rank_dev), axis=1)
    partial_value = local_image.reshape(4, blk_count, pixels // blk_count)
    received = lax.all_to_all(partial_value, "blk", split_axis=1, concat_axis=1, tiled=True)
    group_depths = lax.dynamic_slice_in_dim(device_depth, tri_index * blk_count, blk_count)
    position = (group_depths - jnp.min(group_depths)) // rank_dev
    inverse = (
        jnp.zeros((blk_count,), jnp.int32).at[position].set(jnp.arange(blk_count, dtype=jnp.int32))
    )
    ordered = jnp.take(received, inverse, axis=1)
    own_block = blend_ordered(ordered)
    group_devices = jnp.arange(tri_count, dtype=jnp.int32) * blk_count + blk_index
    tri_depths = device_depth[group_devices]
    gathered = lax.all_gather(own_block[:, None, :], "tri", axis=1, tiled=True)
    composite = blend_group(gathered, tri_depths)
    return composite


def solution(mesh):
    in_specs = (P(("tri", "blk"), None, None), P(("tri", "blk"), None, None), P())
    out_specs = P(None, "blk")
    return jax.shard_map(
        on_device, mesh=mesh, in_specs=in_specs, out_specs=out_specs, check_vma=False
    )
```

profile of v0, /device:TPU:0, one launch (start us, length us, event | category | flops | bytes accessed | tf_op | source)
XLA Modules:
  0.0 224.3 jit_solution(562508941444263034)
XLA Ops:
  0.0 0.8 dynamic_slice.7
  0.8 0.6 fusion.29
  8.9 0.7 convert_element_type.3
  9.6 0.4 mul.178
  10.0 14.3 %copy.26 = f32[1,3,3072,128]{3,1,2,0:T(4,128)} copy(f32[1,3,3072,128]{3,2,1,0:T(8,128)S(1)} %bitcast.97) | data formatting | bytes 9437184
  24.3 19.1 %multiply_bitcast_fusion = f32[4,3,393216]{2,0,1:T(4,128)} fusion(f32[3,4,393216]{2,1,0:T(4,128)} %param.3, f32[3,393216]{1,0:T(4,128)} %bitcast.96), kind=kLoop, calls=%fused_computation.3 | loop fusion | flops 4718592 | bytes 42467328 | tf_op jit(solution)/shard_map/transpose | solution.py:51
  43.4 13.8 %fusion.23 = (f32[4,1,393216]{2,0,1:T(4,128)}, f32[4,1,393216]{2,0,1:T(4,128)}, f32[4,1,393216]{2,0,1:T(4,128)}) fusion(f32[4,3,393216]{2,0,1:T(4,128)} %multiply_bitcast_fusion), kind=kLoop, calls=%fused_computation.69 | loop fusion | bytes 37748736 | tf_op jit(solution)/shard_map/slice | solution.py:31
  57.3 22.5 %fusion.1 = (f32[393216]{0:T(1024)S(1)}, f32[393216]{0:T(1024)}, f32[393216]{0:T(1024)}) fusion(pred[]{:T(512)} %bitcast.2, pred[]{:T(512)} %bitcast.4, f32[4,3,393216]{2,0,1:T(4,128)} %multiply_bitcast_fusion, pred[]{:T(512)} %bitcast.10, pred[]{:T(512)} %bitcast.9, pred[]{:T(512)} %bitcast.7, pred[]{:T(512)} %bitcast.6), kind=kLoop, calls=%fused_computation.15 | loop fusion | flops 4718592 | bytes 9437190 | tf_op jit(solution)/shard_map/mul | solution.py:28
  79.7 0.2 mul.183
  79.9 1.6 mul.187
  81.5 2.6 %mul.191 = f32[64,6144]{1,0:T(8,128)} reshape(f32[393216]{0:T(1024)} %get-tuple-element.6) | data formatting | bytes 3145728 | tf_op jit(solution)/shard_map/mul | solution.py:28
  84.1 12.7 %multiply_add_fusion = f32[4,64,6144]{2,0,1:T(4,128)} fusion(f32[4,64,6144]{2,0,1:T(4,128)} %bitcast.93, f32[4,64,6144]{2,0,1:T(4,128)} %bitcast.94, f32[4,64,6144]{2,0,1:T(4,128)} %bitcast.92, f32[64,6144]{1,0:T(8,128)} %mul.191, f32[64,6144]{1,0:T(8,128)S(1)} %mul.187, f32[64,6144]{1,0:T(8,128)S(1)} %mul.183), kind=kLoop, calls=%fused_computation.6 | loop fusion | flops 7864320 | bytes 29884416 | tf_op jit(solution)/shard_map/add | solution.py:31
  96.8 0.0 copy-start
  96.8 10.4 %all-to-all-start = ((f32[4,64,6144]{2,0,1:T(4,128)}), f32[4,64,6144]{2,0,1:T(4,128)}, u32[]{:S(2)}, u32[]{:S(2)}) async-start(f32[4,64,6144]{2,0,1:T(4,128)} %multiply_add_fusion), calls=%async_computation | async-start | bytes 12582912 | tf_op jit(solution)/shard_map/all_to_all | solution.py:54
  107.2 0.0 copy-done
  107.2 0.2 reshape.295
  107.4 0.1 reduce_min.18
  107.5 0.6 gather_fusion
  108.2 0.6 fusion.28
  111.3 0.7 dynamic-slice_reduce_fusion
  112.0 0.7 compare_select_fusion.1
  112.7 0.8 scatter_custom_fusion
  113.5 0.1 broadcast_in_dim.35
  113.6 0.1 copy.11
  113.8 71.6 %all-to-all-done = f32[4,64,6144]{2,0,1:T(4,128)} async-done(((f32[4,64,6144]{2,0,1:T(4,128)}), f32[4,64,6144]{2,0,1:T(4,128)}, u32[]{:S(2)}, u32[]{:S(2)}) %all-to-all-start) | async-done | bytes 6291488 | tf_op jit(solution)/shard_map/all_to_all | solution.py:54
  185.4 9.4 %gather_fusion.1 = f32[64,4,6144]{2,1,0:T(4,128)} fusion(f32[4,64,6144]{2,0,1:T(4,128)} %all-to-all-done, s32[1024]{0:T(1024)S(1)} %pad_clamp_fusion), kind=kCustom, calls=%fused_computation.1 | custom fusion | bytes 12583168 | tf_op jit(solution)/shard_map/jit(_take)/gather | solution.py:60
  194.7 4.5 %copy_select_fusion = f32[4,32,2,6144]{3,0,1,2:T(4,128)S(1)} fusion(f32[4,32,2,6144]{3,0,2,1:T(4,128)} %bitcast.95, pred[32,2]{0,1:T(4,128)(4,1)S(1)} %copy.11), kind=kLoop, calls=%fused_computation.5 | loop fusion | flops 1572864 | bytes 12582976 | tf_op jit(solution)/shard_map/jit(_take)/select_n | solution.py:60
  199.2 2.1 fusion.24
  201.3 3.3 %fusion.7 = f32[32,6144]{1,0:T(8,128)} fusion(f32[4,32,2,6144]{3,0,1,2:T(4,128)S(1)} %copy_select_fusion), kind=kLoop, calls=%fused_computation.26 | loop fusion | flops 196608 | bytes 1572864 | tf_op jit(solution)/shard_map/sub | solution.py:11
  204.6 2.5 %sub.154 = f32[16,2,6144]{2,1,0:T(2,128)} reshape(f32[32,6144]{1,0:T(8,128)} %fusion.7) | data formatting | bytes 1572864 | tf_op jit(solution)/shard_map/sub | solution.py:11
  207.1 3.3 %multiply_add_fusion.1 = f32[4,16,2,6144]{3,0,2,1:T(4,128)S(1)} fusion(f32[4,16,2,6144]{3,0,2,1:T(4,128)} %bitcast.99, f32[4,16,2,6144]{3,0,2,1:T(4,128)S(1)} %bitcast.98, f32[16,2,6144]{2,1,0:T(2,128)} %sub.154), kind=kLoop, calls=%fused_computation.7 | loop fusion | flops 1572864 | bytes 10223616 | tf_op jit(solution)/shard_map/add | solution.py:11
  210.4 0.2 fusion.25
  210.6 1.9 fusion.9
  212.6 1.2 sub.157
  213.8 0.9 fusion.6
  214.6 0.1 fusion.26
  214.8 0.6 fusion.13
  215.4 0.1 sub.160
  215.5 0.3 fusion.8
  215.8 0.1 fusion.27
  215.9 0.3 fusion.19
  216.2 0.1 sub.163
  216.3 0.1 fusion.10
  216.4 0.1 slice_subtract_fusion.7
  216.5 0.1 fusion.12
  216.7 6.8 %all_gather.3 = f32[4,2,6144]{2,0,1:T(4,128)S(1)} all-gather(f32[4,1,6144]{2,0,1:T(4,128)S(1)} %fusion.18), channel_id=1, replica_groups=mesh['tri'=2,'blk'=64] {'tri'}, dimensions={1}, use_global_device_ids=true | all-gather | bytes 294912 | tf_op jit(solution)/shard_map/all_gather | solution.py:64
  223.5 0.1 broadcast_select_fusion.7
  223.6 0.7 fusion.15
  (10 shorter events, 0.1 us)
Async XLA Ops:
  96.8 10.4 %copy-start = (s32[384]{0:T(512)S(1)}, s32[384]{0:T(512)}, u32[]{:S(2)}) copy-start(s32[384]{0:T(512)} %param.5) | copy-start | bytes 4612
  96.8 88.6 %all-to-all-start = ((f32[4,64,6144]{2,0,1:T(4,128)}), f32[4,64,6144]{2,0,1:T(4,128)}, u32[]{:S(2)}, u32[]{:S(2)}) async-start(f32[4,64,6144]{2,0,1:T(4,128)} %multiply_add_fusion), calls=%async_computation | async-start | bytes 12582912 | tf_op jit(solution)/shard_map/all_to_all | solution.py:54
where the time goes:
time: 228 us; the launch traced here: 224 us
  other arithmetic  72.7 us (32%)
  waiting for transfers between devices  71.6 us (31%)
  local copies, waits for them, and re-layouts  52.4 us (23%)
  starting transfers between devices  10.4 us (5%)
  between operations  10.4 us (5%)
  blocking collectives  6.79 us (3%)
    all_to_all x1, waiting for transfers between devices, on_device(): lax.all_to_all(partial_value, 'blk', split_axis=1, concat_axis=1, tiled=T...  71.6 us
    mul x1, other arithmetic, blend_group(): through * jnp.where(depths[other] < depths[source], 1.0 - stacked[3, othe...  22.5 us
    transpose x1, other arithmetic, on_device(): local_image = blend_group(jnp.moveaxis(masked, 0, 1), own_depths)  19.1 us
    unnamed x5, local copies, waits for them, and re-layouts  14.4 us
    slice x1, local copies, waits for them, and re-layouts, blend_group(): summed = summed + through[None] * stacked[:, source]  13.8 us
    add x2, other arithmetic, blend_group(): summed = summed + through[None] * stacked[:, source]  13.4 us
    all_to_all x1, starting transfers between devices, on_device(): lax.all_to_all(partial_value, 'blk', split_axis=1, concat_axis=1, tiled=T...  10.4 us
    gather x1, local copies, waits for them, and re-layouts, on_device(): ordered = jnp.take(received, inverse, axis=1)  9.36 us
  transfers between devices with their start and end apart: 1, of which 1 were waited for; matrix products, arithmetic and copies ran while one was open for 2% of the time, Pallas kernels for 0%

commit v1 on v0

v1 whole, which is shorter than its diff:
```python
import functools

import jax
import jax.numpy as jnp
from jax import lax
from jax.experimental import pallas as pl
from jax.experimental.pallas import tpu as pltpu
from jax.sharding import PartitionSpec as P

MESH = pl.DeviceIdType.MESH
RANK_DEV = 3
CHANNELS = 4
COLUMN_TILES = 24
BLOCKS = 64
BLOCK_TILES = 48
CHUNK_TILES = 8
CHUNKS = BLOCK_TILES // CHUNK_TILES
ROWS = CHANNELS * CHUNK_TILES


def nearer(depth, left, right):
    return jnp.where(depth[RANK_DEV * left] < depth[RANK_DEV * right], 1.0, 0.0).astype(jnp.float32)


def over(a, b, a_front, b_front):
    through_a = 1.0 - b_front * b[3]
    through_b = 1.0 - a_front * a[3]
    return [through_a * a[ch] + through_b * b[ch] for ch in range(CHANNELS)]


def kernel(layers, tile_mask, depth, out,
           inb, local, from_core, chip, from_pair, pair, from_cross, quad, gathered, outv,
           in_sem, core_send, core_recv, pair_send, pair_recv, cross_send, cross_recv,
           plane_send, plane_recv, out_sem):
    tri = lax.axis_index("tri")
    blk = lax.axis_index("blk")
    core = blk % 2
    z = (blk // 2) % 4
    x = (blk // 8) % 2
    y = blk // 16
    spot = y * 2 + x
    me = tri * BLOCKS + blk
    half = (z % 2 + z // 2) % 2
    item = z // 2

    def device(t, yy, xx, zz, cc):
        return (t, yy * 16 + xx * 8 + zz * 2 + cc)

    core_peer = device(tri, y, x, z, 1 - core)
    pair_peer = device(tri, y, x, z + 1 - 2 * (z % 2), core)
    cross_peer = device(tri, y, x, 3 - z, core)

    def plane_peer(step):
        return (tri + step // 8) % 2, (y + (step // 2) % 4) % 4, (x + step % 2) % 2

    def load_copy(k):
        return pltpu.make_async_copy(
            layers.at[:, :, pl.ds(ROWS * k, ROWS), :], inb.at[k], in_sem.at[k])

    def core_copy(k):
        return pltpu.make_async_remote_copy(
            src_ref=local.at[k, 1 - core], dst_ref=from_core.at[k],
            send_sem=core_send.at[k], recv_sem=core_recv.at[k],
            device_id=core_peer, device_id_type=MESH)

    def pair_copy(k):
        return pltpu.make_async_remote_copy(
            src_ref=chip.at[k, 1 - half], dst_ref=from_pair.at[k],
            send_sem=pair_send.at[k], recv_sem=pair_recv.at[k],
            device_id=pair_peer, device_id_type=MESH)

    def cross_copy(k):
        return pltpu.make_async_remote_copy(
            src_ref=pair.at[k, 1 - item], dst_ref=from_cross.at[k],
            send_sem=cross_send.at[k], recv_sem=cross_recv.at[k],
            device_id=cross_peer, device_id_type=MESH)

    def plane_copy(k, step):
        t, yy, xx = plane_peer(step)
        return pltpu.make_async_remote_copy(
            src_ref=quad.at[k, yy * 2 + xx], dst_ref=gathered.at[k, tri * 8 + spot],
            send_sem=plane_send.at[k, step], recv_sem=plane_recv.at[k, tri * 8 + spot],
            device_id=device(t, yy, xx, z, core), device_id_type=MESH)

    def plane_arrival(k, step):
        t, yy, xx = plane_peer(step)
        source = t * 8 + yy * 2 + xx
        return pltpu.make_async_remote_copy(
            src_ref=quad.at[k, spot], dst_ref=gathered.at[k, source],
            send_sem=plane_send.at[k, step], recv_sem=plane_recv.at[k, source],
            device_id=device(t, yy, xx, z, core), device_id_type=MESH)

    for k in range(CHUNKS):
        load_copy(k).start()

    barrier = pltpu.get_barrier_semaphore()
    for peer in (core_peer, pair_peer, cross_peer):
        pl.semaphore_signal(barrier, inc=1, device_id=peer, device_id_type=MESH)

    @pl.loop(1, 16)
    def _(step):
        t, yy, xx = plane_peer(step)
        pl.semaphore_signal(barrier, inc=1, device_id=device(t, yy, xx, z, core), device_id_type=MESH)

    own = [depth[RANK_DEV * me + r] for r in range(RANK_DEV)]
    front = [[jnp.where(own[j] < own[r], 1.0, 0.0).astype(jnp.float32) for r in range(RANK_DEV)]
             for j in range(RANK_DEV)]

    def flags(peer):
        other = peer[0] * BLOCKS + peer[1]
        return nearer(depth, me, other), nearer(depth, other, me)

    core_flags = flags(core_peer)
    pair_flags = flags(pair_peer)
    cross_flags = flags(cross_peer)

    sub = lax.broadcasted_iota(jnp.int32, (CHUNK_TILES, 128), 0)

    def mask_of(r, group):
        value = jnp.zeros((CHUNK_TILES, 128), jnp.float32)
        for s in range(CHUNK_TILES):
            on = tile_mask[r, 0, CHUNK_TILES * group + s].astype(jnp.float32)
            value = jnp.where(sub == s, on, value)
        return value

    masks = [[mask_of(r, g) for r in range(RANK_DEV)] for g in range(COLUMN_TILES // CHUNK_TILES)]

    def blend_local(k, to_core):
        mask = masks[k % (COLUMN_TILES // CHUNK_TILES)]

        @pl.loop(0, 32)
        def _(n):
            hh, ii, pp = n // 16, (n // 8) % 2, n % 8
            zz = hh + ii * (3 - 2 * hh)
            b = pp * 8 + zz * 2 + to_core

            def plane(r, ch):
                return inb[k, r, b, pl.ds(ch, CHUNK_TILES, stride=CHANNELS), :]

            opacity = [mask[r] * plane(r, 3) for r in range(RANK_DEV)]
            weights = []
            for r in range(RANK_DEV):
                weight = mask[r]
                for j in range(RANK_DEV):
                    if j != r:
                        weight = weight * (1.0 - front[j][r] * opacity[j])
                weights.append(weight)
            for ch in range(CHANNELS):
                total = weights[0] * plane(0, ch)
                for r in range(1, RANK_DEV):
                    total = total + weights[r] * plane(r, ch)
                local[k, to_core, hh, ii, pp, ch] = total

    def blend_chip(k, to_half):
        @pl.loop(0, 16)
        def _(n):
            ii, pp = n // 8, n % 8
            a = [local[k, core, to_half, ii, pp, ch] for ch in range(CHANNELS)]
            b = [from_core[k, to_half, ii, pp, ch] for ch in range(CHANNELS)]
            for ch, value in enumerate(over(a, b, *core_flags)):
                chip[k, to_half, ii, pp, ch] = value

    def blend_pair(k, to_item):
        @pl.loop(0, 8)
        def _(pp):
            a = [chip[k, half, to_item, pp, ch] for ch in range(CHANNELS)]
            b = [from_pair[k, to_item, pp, ch] for ch in range(CHANNELS)]
            for ch, value in enumerate(over(a, b, *pair_flags)):
                pair[k, to_item, pp, ch] = value

    def blend_cross(k):
        @pl.loop(0, 8)
        def _(pp):
            a = [pair[k, item, pp, ch] for ch in range(CHANNELS)]
            b = [from_cross[k, pp, ch] for ch in range(CHANNELS)]
            for ch, value in enumerate(over(a, b, *cross_flags)):
                quad[k, pp, ch] = value

        for ch in range(CHANNELS):
            gathered[k, tri * 8 + spot, ch] = quad[k, spot, ch]

    def quad_device(q):
        return (q // 8) * BLOCKS + (q % 8) * 8

    plane_flags = []
    span = 1
    while span < 16:
        plane_flags.append([
            (nearer(depth, quad_device(q), quad_device(q + span)),
             nearer(depth, quad_device(q + span), quad_device(q)))
            for q in range(0, 16, 2 * span)])
        span *= 2

    def blend_plane(k):
        images = [[gathered[k, q, ch] for ch in range(CHANNELS)] for q in range(16)]
        for level in plane_flags:
            images = [over(images[2 * n], images[2 * n + 1], *level[n]) for n in range(len(level))]
        for ch in range(CHANNELS):
            outv[pl.ds(ROWS * k + ch, CHUNK_TILES, stride=CHANNELS), :] = images[0][ch]

    def first_stage(k):
        load_copy(k).wait()
        blend_local(k, 1 - core)
        if k == 0:
            pl.semaphore_wait(barrier, 18)
        core_copy(k).start()
        blend_local(k, core)

    def second_stage(k):
        core_copy(k).wait_recv()
        blend_chip(k, 1 - half)
        pair_copy(k).start()
        blend_chip(k, half)

    def third_stage(k):
        pair_copy(k).wait_recv()
        blend_pair(k, 1 - item)
        cross_copy(k).start()
        blend_pair(k, item)

    def fourth_stage(k):
        cross_copy(k).wait_recv()
        blend_cross(k)

        @pl.loop(1, 16)
        def _(step):
            plane_copy(k, step).start()

    def last_stage(k):
        @pl.loop(1, 16)
        def _(step):
            plane_arrival(k, step).wait_recv()

        blend_plane(k)

    first_stage(0)
    for k in range(1, CHUNKS):
        first_stage(k)
        second_stage(k - 1)
    second_stage(CHUNKS - 1)
    for k in range(CHUNKS):
        third_stage(k)
        if k >= 1:
            fourth_stage(k - 1)
        if k >= 2:
            last_stage(k - 2)
    fourth_stage(CHUNKS - 1)
    last_stage(CHUNKS - 2)
    last_stage(CHUNKS - 1)
    result = pltpu.make_async_copy(outv, out, out_sem)
    result.start()
    for k in range(CHUNKS):
        core_copy(k).wait_send()
        pair_copy(k).wait_send()
        cross_copy(k).wait_send()

        @pl.loop(1, 16)
        def _(step):
            plane_copy(k, step).wait_send()
    result.wait()


def on_device(layers, tile_mask, depth_order):
    rank_dev, channels, pixels = layers.shape
    tiles = pixels // 128
    rows = layers.reshape(rank_dev, channels, tiles, 128).transpose(0, 2, 1, 3)
    rows = rows.reshape(rank_dev, BLOCKS, BLOCK_TILES * channels, 128)
    image = (CHANNELS, CHUNK_TILES, 128)
    dma = pltpu.SemaphoreType.DMA
    out = pl.pallas_call(
        kernel,
        out_shape=jax.ShapeDtypeStruct((BLOCK_TILES * channels, 128), jnp.float32),
        in_specs=[
            pl.BlockSpec(memory_space=pl.ANY),
            pl.BlockSpec(memory_space=pltpu.SMEM),
            pl.BlockSpec(memory_space=pltpu.SMEM),
        ],
        out_specs=pl.BlockSpec(memory_space=pl.ANY),
        scratch_shapes=[
            pltpu.VMEM((CHUNKS, rank_dev, BLOCKS, ROWS, 128), jnp.float32),
            pltpu.VMEM((CHUNKS, 2, 2, 2, 8) + image, jnp.float32),
            pltpu.VMEM((CHUNKS, 2, 2, 8) + image, jnp.float32),
            pltpu.VMEM((CHUNKS, 2, 2, 8) + image, jnp.float32),
            pltpu.VMEM((CHUNKS, 2, 8) + image, jnp.float32),
            pltpu.VMEM((CHUNKS, 2, 8) + image, jnp.float32),
            pltpu.VMEM((CHUNKS, 8) + image, jnp.float32),
            pltpu.VMEM((CHUNKS, 8) + image, jnp.float32),
            pltpu.VMEM((CHUNKS, 16) + image, jnp.float32),
            pltpu.VMEM((BLOCK_TILES * channels, 128), jnp.float32),
            dma((CHUNKS,)),
            dma((CHUNKS,)), dma((CHUNKS,)),
            dma((CHUNKS,)), dma((CHUNKS,)),
            dma((CHUNKS,)), dma((CHUNKS,)),
            dma((CHUNKS, 16)), dma((CHUNKS, 16)),
            dma,
        ],
        compiler_params=pltpu.CompilerParams(
            collective_id=0, has_side_effects=True, vmem_limit_bytes=60 * 1024 * 1024),
    )(rows, tile_mask, depth_order)
    out = out.reshape(BLOCK_TILES, channels, 128).transpose(1, 0, 2)
    return out.reshape(channels, BLOCK_TILES * 128)


def solution(mesh):
    in_specs = (P(("tri", "blk"), None, None), P(("tri", "blk"), None, None), P())
    out_specs = P(None, "blk")
    return jax.shard_map(
        on_device, mesh=mesh, in_specs=in_specs, out_specs=out_specs, check_vma=False
    )
```

time: 228 us -> 61.2 us (0.27); the launches traced: 224 us -> 61.1 us
  other arithmetic: 72.7 us -> 0 us
  waiting for transfers between devices: 71.6 us -> 0 us
  Pallas kernels: 0 us -> 59.5 us
  local copies, waits for them, and re-layouts: 52.4 us -> 1.54 us
  starting transfers between devices: 10.4 us -> 0 us
  between operations: 10.4 us -> 0.01 us
  blocking collectives: 6.79 us -> 0 us
    all_to_all x1 -> x0, waiting for transfers between devices: 71.6 us -> none  [on_device(): lax.all_to_all(partial_value, 'blk', split_axis=1, concat_axis=1, tiled=T...]
    pallas_call x0 -> x1, Pallas kernels: none -> 59.5 us  [on_device(): pl.pallas_call(kernel, out_shape=jax.ShapeDtypeStruct((BLOCK_TILES * chan...]
    mul x1 -> x0, other arithmetic: 22.5 us -> none  [blend_group(): through * jnp.where(depths[other] < depths[source], 1.0 - stacked[3, othe...]
    transpose x1 -> x0, other arithmetic: 19.1 us -> none  [on_device(): local_image = blend_group(jnp.moveaxis(masked, 0, 1), own_depths)]
    add x8 -> x0, other arithmetic: 18 us -> none  [the longest x2 13.4 us: blend_group(): summed = summed + through[None] * stacked[:, source]]
    slice x7 -> x0, local copies, waits for them, and re-layouts: 17.5 us -> none  [the longest x1 13.8 us: blend_group(): summed = summed + through[None] * stacked[:, source]]
    unnamed x5 -> x1, local copies, waits for them, and re-layouts: 14.4 us -> 1.54 us
    all_to_all x1 -> x0, starting transfers between devices: 10.4 us -> none  [on_device(): lax.all_to_all(partial_value, 'blk', split_axis=1, concat_axis=1, tiled=T...]
  transfers between devices with their start and end apart: 1 -> 0, of which waited for: 1 -> 0; matrix products, arithmetic and copies ran while one was open for 2% -> 0% of each run, Pallas kernels for 0% -> 0%
where the time goes in v1:
time: 61.2 us; the launch traced here: 61.1 us
  Pallas kernels  59.5 us (97%)
  local copies, waits for them, and re-layouts  1.54 us (3%)
    pallas_call x1, Pallas kernels, on_device(): pl.pallas_call(kernel, out_shape=jax.ShapeDtypeStruct((BLOCK_TILES * chan...  59.5 us
    unnamed x1, local copies, waits for them, and re-layouts  1.54 us

profile of v1, /device:TPU:0, one launch (start us, length us, event | category | flops | bytes accessed | tf_op | source)
XLA Modules:
  0.0 61.1 jit_solution(5187483182266552970)
XLA Ops:
  0.0 59.5 %shard_map.37 = f32[192,128]{1,0:T(8,128)} custom-call(f32[3,64,192,128]{3,2,1,0:T(8,128)} %bitcast.10, s32[3,1,24]{2,1,0:T(1,128)} %tile_mask.1, s32[384]{0:T(512)} %depth.1), custom_call_target="tpu_custom_call" | custom-call | tf_op jit(solution)/shard_map/pallas_call | solution.py:270
  59.5 1.5 %copy.7 = f32[4,6144]{1,0:T(4,128)} copy(f32[4,6144]{1,0:T(4,128)} %bitcast.11) | data formatting | bytes 196608

commit v2 on v0

v2 whole, which is shorter than its diff:
```python
import jax
import jax.numpy as jnp
from jax import lax
from jax.experimental import pallas as pl
from jax.experimental.pallas import tpu as pltpu
from jax.sharding import PartitionSpec as P

MESH = pl.DeviceIdType.MESH
RANK_DEV = 3
CHANNELS = 4
COLUMN_TILES = 24
BLOCKS = 64
BLOCK_TILES = 48
CHUNK_TILES = 8
CHUNKS = BLOCK_TILES // CHUNK_TILES
ROWS = CHANNELS * CHUNK_TILES
SPOTS = 8
UNITS = ((0, 0, 1), (0, 1, 1), (0, 2, 2), (1, 0, 4), (2, 0, 4), (3, 0, 4), (4, 0, 4),
         (5, 0, 2), (5, 2, 1), (5, 3, 1))


def spot_of(y, x):
    return 4 * ((y + x) % 2) + 2 * x + y // 2


def place_of(spot):
    x = (spot // 2) % 2
    return 2 * (spot % 2) + (x + spot // 4) % 2, x


def over(a, b, a_front, b_front):
    through_a = 1.0 - b_front * b[3]
    through_b = 1.0 - a_front * a[3]
    return [through_a * a[ch] + through_b * b[ch] for ch in range(CHANNELS)]


def kernel(layers, mask_in, depth_in, out,
           inb, local, from_core, chip, from_pair, pair, from_cross, quad, gathered, outv,
           tile_mask, depth,
           in_sem, core_send, core_recv, pair_send, pair_recv, cross_send, cross_recv,
           plane_send, plane_recv, small_sem):
    tri = lax.axis_index("tri")
    blk = lax.axis_index("blk")
    core = blk % 2
    z = (blk // 2) % 4
    x = (blk // 8) % 2
    y = blk // 16
    spot = spot_of(y, x)
    me = tri * BLOCKS + blk
    half = (z % 2 + z // 2) % 2
    item = z // 2

    def device(t, yy, xx, zz, cc):
        return (t, yy * 16 + xx * 8 + zz * 2 + cc)

    core_peer = device(tri, y, x, z, 1 - core)
    pair_peer = device(tri, y, x, z + 1 - 2 * (z % 2), core)
    cross_peer = device(tri, y, x, 3 - z, core)

    def load_copy(u, m):
        k, first, _ = UNITS[u]
        low = (m % 2 + m // 2) % 2 * 2 + m % 2
        return pltpu.make_async_copy(
            layers.at[:, :, low, :, pl.ds(ROWS * k, ROWS), :], inb.at[k, m], in_sem.at[u])

    def load_wait(u):
        k, first, count = UNITS[u]
        pltpu.make_async_copy(
            inb.at[k, pl.ds(first, count)], inb.at[k, pl.ds(first, count)], in_sem.at[u]).wait()

    def load_start(u):
        k, first, count = UNITS[u]
        for m in range(first, first + count):
            load_copy(u, m).start()

    def spots(u):
        k, first, count = UNITS[u]
        return k, pl.ds(2 * first, 2 * count)

    def core_copy(u):
        k, part = spots(u)
        return pltpu.make_async_remote_copy(
            src_ref=local.at[k, 1 - core, :, :, part], dst_ref=from_core.at[k, :, :, part],
            send_sem=core_send.at[u], recv_sem=core_recv.at[u],
            device_id=core_peer, device_id_type=MESH)

    def pair_copy(u):
        k, part = spots(u)
        return pltpu.make_async_remote_copy(
            src_ref=chip.at[k, 1 - half, :, part], dst_ref=from_pair.at[k, :, part],
            send_sem=pair_send.at[u], recv_sem=pair_recv.at[u],
            device_id=pair_peer, device_id_type=MESH)

    def cross_copy(u):
        k, part = spots(u)
        return pltpu.make_async_remote_copy(
            src_ref=pair.at[k, 1 - item, part], dst_ref=from_cross.at[k, part],
            send_sem=cross_send.at[u], recv_sem=cross_recv.at[u],
            device_id=cross_peer, device_id_type=MESH)

    def plane_copy(k, t, other):
        yy, xx = place_of(other)
        return pltpu.make_async_remote_copy(
            src_ref=quad.at[k, other], dst_ref=gathered.at[k, tri * SPOTS + spot],
            send_sem=plane_send.at[k], recv_sem=plane_recv.at[k],
            device_id=device(t, yy, xx, z, core), device_id_type=MESH)

    def plane_all(k):
        return pltpu.make_async_remote_copy(
            src_ref=gathered.at[k, pl.ds(0, 2 * SPOTS - 1)],
            dst_ref=gathered.at[k, pl.ds(0, 2 * SPOTS - 1)],
            send_sem=plane_send.at[k], recv_sem=plane_recv.at[k],
            device_id=core_peer, device_id_type=MESH)

    mask_copy = pltpu.make_async_copy(mask_in, tile_mask, small_sem.at[0])
    depth_copy = pltpu.make_async_copy(depth_in, depth, small_sem.at[1])
    mask_copy.start()
    depth_copy.start()
    load_start(0)
    load_start(1)

    barrier = pltpu.get_barrier_semaphore()
    for peer in (core_peer, pair_peer, cross_peer):
        pl.semaphore_signal(barrier, inc=1, device_id=peer, device_id_type=MESH)
    for step in range(1, 2 * SPOTS):
        t = (tri + step // SPOTS) % 2
        yy, xx = place_of((spot + step) % SPOTS)
        pl.semaphore_signal(barrier, inc=1, device_id=device(t, yy, xx, z, core), device_id_type=MESH)

    for u in range(2, len(UNITS)):
        load_start(u)
    mask_copy.wait()
    depth_copy.wait()

    def nearer(left, right):
        return jnp.where(
            depth[RANK_DEV * left] < depth[RANK_DEV * right], 1.0, 0.0).astype(jnp.float32)

    own = [depth[RANK_DEV * me + r] for r in range(RANK_DEV)]
    front = [[jnp.where(own[j] < own[r], 1.0, 0.0).astype(jnp.float32) for r in range(RANK_DEV)]
             for j in range(RANK_DEV)]

    def flags(peer):
        other = peer[0] * BLOCKS + peer[1]
        return nearer(me, other), nearer(other, me)

    core_flags = flags(core_peer)
    pair_flags = flags(pair_peer)
    cross_flags = flags(cross_peer)

    def quad_device(q):
        yy, xx = (q // 2) % 4, q % 2
        return (q // 8) * BLOCKS + yy * 16 + xx * 8

    plane_flags = []
    span = 1
    while span < 2 * SPOTS:
        plane_flags.append([
            (nearer(quad_device(q), quad_device(q + span)),
             nearer(quad_device(q + span), quad_device(q)))
            for q in range(0, 2 * SPOTS, 2 * span)])
        span *= 2

    sub = lax.broadcasted_iota(jnp.int32, (CHUNK_TILES, 128), 0)

    def mask_of(r, group):
        value = jnp.zeros((CHUNK_TILES, 128), jnp.float32)
        for s in range(CHUNK_TILES):
            on = tile_mask[r, 0, CHUNK_TILES * group + s].astype(jnp.float32)
            value = jnp.where(sub == s, on, value)
        return value

    masks = [[mask_of(r, g) for r in range(RANK_DEV)] for g in range(COLUMN_TILES // CHUNK_TILES)]

    def blend_local(u, to_core):
        k, first, count = UNITS[u]
        mask = masks[k % (COLUMN_TILES // CHUNK_TILES)]
        for hh in range(2):
            for ii in range(2):
                block = (hh + ii * (3 - 2 * hh)) * 2 + to_core

                @pl.loop(2 * first, 2 * (first + count), unroll=2)
                def _(o):
                    def plane(r, ch):
                        return inb[k, o // 2, r, o % 2, block,
                                   pl.ds(ch, CHUNK_TILES, stride=CHANNELS), :]

                    opacity = [mask[r] * plane(r, 3) for r in range(RANK_DEV)]
                    weights = []
                    for r in range(RANK_DEV):
                        weight = mask[r]
                        for j in range(RANK_DEV):
                            if j != r:
                                weight = weight * (1.0 - front[j][r] * opacity[j])
                        weights.append(weight)
                    for ch in range(CHANNELS):
                        total = weights[0] * plane(0, ch)
                        for r in range(1, RANK_DEV):
                            total = total + weights[r] * plane(r, ch)
                        local[k, to_core, hh, ii, o, ch] = total

    def blend_chip(u, to_half):
        k, first, count = UNITS[u]
        for ii in range(2):
            @pl.loop(2 * first, 2 * (first + count), unroll=2)
            def _(o):
                a = [local[k, core, to_half, ii, o, ch] for ch in range(CHANNELS)]
                b = [from_core[k, to_half, ii, o, ch] for ch in range(CHANNELS)]
                for ch, value in enumerate(over(a, b, *core_flags)):
                    chip[k, to_half, ii, o, ch] = value

    def blend_pair(u, to_item):
        k, first, count = UNITS[u]

        @pl.loop(2 * first, 2 * (first + count), unroll=2)
        def _(o):
            a = [chip[k, half, to_item, o, ch] for ch in range(CHANNELS)]
            b = [from_pair[k, to_item, o, ch] for ch in range(CHANNELS)]
            for ch, value in enumerate(over(a, b, *pair_flags)):
                pair[k, to_item, o, ch] = value

    def blend_cross(u):
        k, first, count = UNITS[u]

        @pl.loop(2 * first, 2 * (first + count), unroll=2)
        def _(o):
            a = [pair[k, item, o, ch] for ch in range(CHANNELS)]
            b = [from_cross[k, o, ch] for ch in range(CHANNELS)]
            for ch, value in enumerate(over(a, b, *cross_flags)):
                quad[k, o, ch] = value

    def blend_plane(k):
        for ch in range(CHANNELS):
            gathered[k, tri * SPOTS + spot, ch] = quad[k, spot, ch]
        images = []
        for q in range(2 * SPOTS):
            slot = (q // SPOTS) * SPOTS + spot_of((q // 2) % 4, q % 2)
            images.append([gathered[k, slot, ch] for ch in range(CHANNELS)])
        for level in plane_flags:
            images = [over(images[2 * n], images[2 * n + 1], *level[n]) for n in range(len(level))]
        for ch in range(CHANNELS):
            outv[pl.ds(ROWS * k + ch, CHUNK_TILES, stride=CHANNELS), :] = images[0][ch]

    def first_stage(u):
        with jax.named_scope(f"w_load{u}"):
            load_wait(u)
        with jax.named_scope(f"c_local{u}"):
            blend_local(u, 1 - core)
        if u == 0:
            with jax.named_scope("w_barrier"):
                pl.semaphore_wait(barrier, 18)
        core_copy(u).start()
        with jax.named_scope(f"c_own{u}"):
            blend_local(u, core)

    def second_stage(u):
        with jax.named_scope(f"w_core{u}"):
            core_copy(u).wait_recv()
        with jax.named_scope(f"c_chip{u}"):
            blend_chip(u, 1 - half)
        pair_copy(u).start()
        with jax.named_scope(f"c_chipown{u}"):
            blend_chip(u, half)

    def third_stage(u):
        with jax.named_scope(f"w_pair{u}"):
            pair_copy(u).wait_recv()
        with jax.named_scope(f"c_pair{u}"):
            blend_pair(u, 1 - item)
        cross_copy(u).start()
        with jax.named_scope(f"c_pairown{u}"):
            blend_pair(u, item)

    def fourth_stage(u):
        k, first, count = UNITS[u]
        with jax.named_scope(f"w_cross{u}"):
            cross_copy(u).wait_recv()
        with jax.named_scope(f"c_cross{u}"):
            blend_cross(u)
        with jax.named_scope(f"s_plane{u}"):
            for step in range(4 * count):
                t = (tri + 1 + step // (2 * count)) % 2
                other = 2 * first + (spot + step) % (2 * count)

                @pl.when((t != tri) | (other != spot))
                def _():
                    plane_copy(k, t, other).start()

    def last_stage(k):
        with jax.named_scope(f"w_plane{k}"):
            plane_all(k).wait_recv()
        with jax.named_scope(f"c_plane{k}"):
            blend_plane(k)

    first_stage(0)
    for u in range(1, len(UNITS)):
        first_stage(u)
        second_stage(u - 1)
    second_stage(len(UNITS) - 1)
    for u in range(len(UNITS)):
        third_stage(u)
        if u >= 1:
            fourth_stage(u - 1)
    fourth_stage(len(UNITS) - 1)
    for k in range(CHUNKS - 1):
        last_stage(k)
    with jax.named_scope("w_sends"):
        for u in range(len(UNITS)):
            core_copy(u).wait_send()
            pair_copy(u).wait_send()
            cross_copy(u).wait_send()
        for k in range(CHUNKS):
            plane_all(k).wait_send()
    last_stage(CHUNKS - 1)
    with jax.named_scope("w_out"):
        result = pltpu.make_async_copy(outv, out, small_sem.at[0])
        result.start()
        result.wait()


def on_device(layers, tile_mask, depth_order):
    rank_dev, channels, pixels = layers.shape
    tiles = pixels // 128
    rows = layers.reshape(rank_dev, channels, tiles, 128).transpose(0, 2, 1, 3)
    rows = rows.reshape(rank_dev, 2, 4, 8, BLOCK_TILES * channels, 128)
    image = (CHANNELS, CHUNK_TILES, 128)
    units = len(UNITS)
    dma = pltpu.SemaphoreType.DMA
    out = pl.pallas_call(
        kernel,
        out_shape=jax.ShapeDtypeStruct((BLOCK_TILES * channels, 128), jnp.float32),
        in_specs=[pl.BlockSpec(memory_space=pltpu.HBM)] * 3,
        out_specs=pl.BlockSpec(memory_space=pl.ANY),
        scratch_shapes=[
            pltpu.VMEM((CHUNKS, 4, rank_dev, 2, 8, ROWS, 128), jnp.float32),
            pltpu.VMEM((CHUNKS, 2, 2, 2, SPOTS) + image, jnp.float32),
            pltpu.VMEM((CHUNKS, 2, 2, SPOTS) + image, jnp.float32),
            pltpu.VMEM((CHUNKS, 2, 2, SPOTS) + image, jnp.float32),
            pltpu.VMEM((CHUNKS, 2, SPOTS) + image, jnp.float32),
            pltpu.VMEM((CHUNKS, 2, SPOTS) + image, jnp.float32),
            pltpu.VMEM((CHUNKS, SPOTS) + image, jnp.float32),
            pltpu.VMEM((CHUNKS, SPOTS) + image, jnp.float32),
            pltpu.VMEM((CHUNKS, 2 * SPOTS) + image, jnp.float32),
            pltpu.VMEM((BLOCK_TILES * channels, 128), jnp.float32),
            pltpu.SMEM(tile_mask.shape, jnp.int32),
            pltpu.SMEM(depth_order.shape, jnp.int32),
            dma((units,)),
            dma((units,)), dma((units,)),
            dma((units,)), dma((units,)),
            dma((units,)), dma((units,)),
            dma((CHUNKS,)), dma((CHUNKS,)),
            dma((2,)),
        ],
        compiler_params=pltpu.CompilerParams(
            collective_id=0, has_side_effects=True, vmem_limit_bytes=60 * 1024 * 1024),
    )(rows, tile_mask, depth_order)
    out = out.reshape(BLOCK_TILES, channels, 128).transpose(1, 0, 2)
    return out.reshape(channels, BLOCK_TILES * 128)


def solution(mesh):
    in_specs = (P(("tri", "blk"), None, None), P(("tri", "blk"), None, None), P())
    out_specs = P(None, "blk")
    return jax.shard_map(
        on_device, mesh=mesh, in_specs=in_specs, out_specs=out_specs, check_vma=False
    )
```

time: 228 us -> 56.8 us (0.25); the launches traced: 224 us -> 55.7 us
  other arithmetic: 72.7 us -> 0 us
  waiting for transfers between devices: 71.6 us -> 0 us
  Pallas kernels: 0 us -> 54.2 us
  local copies, waits for them, and re-layouts: 52.4 us -> 1.54 us
  starting transfers between devices: 10.4 us -> 0 us
  between operations: 10.4 us -> 0.01 us
  blocking collectives: 6.79 us -> 0 us
    all_to_all x1 -> x0, waiting for transfers between devices: 71.6 us -> none  [on_device(): lax.all_to_all(partial_value, 'blk', split_axis=1, concat_axis=1, tiled=T...]
    pallas_call x0 -> x1, Pallas kernels: none -> 54.2 us  [on_device(): pl.pallas_call(kernel, out_shape=jax.ShapeDtypeStruct((BLOCK_TILES * chan...]
    mul x1 -> x0, other arithmetic: 22.5 us -> none  [blend_group(): through * jnp.where(depths[other] < depths[source], 1.0 - stacked[3, othe...]
    transpose x1 -> x0, other arithmetic: 19.1 us -> none  [on_device(): local_image = blend_group(jnp.moveaxis(masked, 0, 1), own_depths)]
    add x8 -> x0, other arithmetic: 18 us -> none  [the longest x2 13.4 us: blend_group(): summed = summed + through[None] * stacked[:, source]]
    slice x7 -> x0, local copies, waits for them, and re-layouts: 17.5 us -> none  [the longest x1 13.8 us: blend_group(): summed = summed + through[None] * stacked[:, source]]
    unnamed x5 -> x1, local copies, waits for them, and re-layouts: 14.4 us -> 1.54 us
    all_to_all x1 -> x0, starting transfers between devices: 10.4 us -> none  [on_device(): lax.all_to_all(partial_value, 'blk', split_axis=1, concat_axis=1, tiled=T...]
  transfers between devices with their start and end apart: 1 -> 0, of which waited for: 1 -> 0; matrix products, arithmetic and copies ran while one was open for 2% -> 0% of each run, Pallas kernels for 0% -> 0%
where the time goes in v2:
time: 56.8 us; the launch traced here: 55.7 us
  Pallas kernels  54.2 us (95%)
  local copies, waits for them, and re-layouts  1.54 us (3%)
    pallas_call x1, Pallas kernels, on_device(): pl.pallas_call(kernel, out_shape=jax.ShapeDtypeStruct((BLOCK_TILES * chan...  54.2 us
    unnamed x1, local copies, waits for them, and re-layouts  1.54 us

profile of v2, /device:TPU:0, one launch (start us, length us, event | category | flops | bytes accessed | tf_op | source)
XLA Modules:
  0.0 55.7 jit_solution(14283176949040043746)
XLA Ops:
  0.0 54.2 %shard_map.37 = f32[192,128]{1,0:T(8,128)} custom-call(f32[3,2,4,8,192,128]{5,4,3,2,1,0:T(8,128)} %bitcast.10, s32[3,1,24]{2,1,0:T(1,128)} %mask_in.1, s32[384]{0:T(512)} %depth_in.1), custom_call_target="tpu_custom_call" | custom-call | tf_op jit(solution)/shard_map/pallas_call | solution.py:329
  54.2 1.5 %copy.7 = f32[4,6144]{1,0:T(4,128)} copy(f32[4,6144]{1,0:T(4,128)} %bitcast.11) | data formatting | bytes 196608

commit v3 on v2

v3 whole, which is shorter than its diff:
```python
import jax
import jax.numpy as jnp
from jax import lax
from jax.experimental import pallas as pl
from jax.experimental.pallas import tpu as pltpu
from jax.sharding import PartitionSpec as P

MESH = pl.DeviceIdType.MESH
RANK_DEV = 3
CHANNELS = 4
COLUMN_TILES = 24
BLOCKS = 64
BLOCK_TILES = 48
CHUNK_TILES = 8
CHUNKS = BLOCK_TILES // CHUNK_TILES
ROWS = CHANNELS * CHUNK_TILES
SPOTS = 8
UNITS = (
    (0, 0, 1, 'P'),
    (0, 1, 1, 'P'),
    (0, 2, 1, 'P'),
    (0, 3, 1, 'P'),
    (1, 0, 4, 'P'),
    (2, 0, 2, 'P'),
    (2, 2, 1, 'T'),
    (2, 3, 1, 'T'),
    (3, 0, 2, 'T'),
    (3, 2, 2, 'T'),
    (4, 0, 4, 'T'),
    (5, 0, 1, 'T'),
    (5, 1, 1, 'T'),
    (5, 2, 1, 'T'),
    (5, 3, 1, 'T'),
)
LOADS = (3, 6, 1, 10, 2, 4, 5, 9, 8, 0, 14, 7, 11, 13, 12)
FAR = (5,)
PLAN = (
    ('L', 3), ('L', 6), ('L', 1), ('L', 10), ('C', 3), ('S', 3), ('C', 6), ('S', 6), ('C', 1),
    ('S', 1), ('L', 2), ('L', 4), ('C', 10), ('S', 10), ('C', 2), ('S', 2), ('L', 5), ('L', 9),
    ('L', 8), ('A', 3), ('A', 6), ('C', 4), ('S', 4), ('C', 5), ('L', 0), ('L', 14), ('C', 9),
    ('L', 7), ('L', 11), ('C', 8), ('A', 1), ('L', 13), ('C', 0), ('L', 12), ('C', 14), ('C', 7),
    ('S', 9), ('C', 11), ('C', 13), ('A', 2), ('C', 12), ('B', 6), ('A', 10), ('S', 8), ('B', 3),
    ('B', 1), ('S', 5), ('S', 14), ('A', 4), ('D', 6), ('A', 9), ('B', 10), ('B', 2), ('S', 7),
    ('A', 5), ('B', 9), ('A', 8), ('A', 14), ('S', 11), ('S', 0), ('D', 10), ('S', 13), ('B', 4),
    ('S', 12), ('D', 9), ('B', 8), ('A', 7), ('B', 14), ('B', 5), ('A', 0), ('A', 11), ('G', 4),
    ('D', 8), ('B', 7), ('A', 13), ('D', 14), ('B', 11), ('G', 1), ('A', 12), ('D', 7), ('B', 13),
    ('B', 0), ('F', 4), ('D', 11), ('B', 12), ('G', 3), ('D', 13), ('F', 1), ('D', 12), ('G', 2),
    ('G', 0), ('F', 3), ('F', 2), ('F', 0), ('F', 5),
)


def spot_of(y, x):
    return 4 * ((y + x) % 2) + 2 * x + y // 2


def place_of(spot):
    x = (spot // 2) % 2
    return 2 * (spot % 2) + (x + spot // 4) % 2, x


def over(a, b, a_front, b_front):
    through_a = 1.0 - b_front * b[3]
    through_b = 1.0 - a_front * a[3]
    return [through_a * a[ch] + through_b * b[ch] for ch in range(CHANNELS)]


def kernel(layers, mask_in, depth_in, out,
           inb, local, from_core, chip, from_pair, pair, from_cross, from_skip, gap, from_gap,
           merged, from_merged, quad, gathered, group, from_group, outv, tile_mask, depth,
           in_sem, core_send, core_recv, first_send, first_recv, second_send, second_recv,
           third_send, third_recv, plane_send, plane_recv, group_send, group_recv, small_sem):
    tri = lax.axis_index("tri")
    blk = lax.axis_index("blk")
    core = blk % 2
    z = (blk // 2) % 4
    x = (blk // 8) % 2
    y = blk // 16
    spot = spot_of(y, x)
    me = tri * BLOCKS + blk
    half = (z % 2 + z // 2) % 2
    item = z // 2

    def device(t, yy, xx, zz, cc):
        return (t, yy * 16 + xx * 8 + zz * 2 + cc)

    core_peer = device(tri, y, x, z, 1 - core)
    pair_peer = device(tri, y, x, z + 1 - 2 * (z % 2), core)
    cross_peer = device(tri, y, x, 3 - z, core)
    skew_peer = device(tri, y, x, (z + 2) % 4, core)
    tri_peer = device(1 - tri, y, x, z, core)

    def load_copy(u, m):
        k, first, _, _ = UNITS[u]
        low = (m % 2 + m // 2) % 2 * 2 + m % 2
        return pltpu.make_async_copy(
            layers.at[:, :, low, :, pl.ds(ROWS * k, ROWS), :], inb.at[k, m], in_sem.at[u])

    def load_wait(u):
        k, first, count, _ = UNITS[u]
        pltpu.make_async_copy(
            inb.at[k, pl.ds(first, count)], inb.at[k, pl.ds(first, count)], in_sem.at[u]).wait()

    def load_start(u):
        k, first, count, _ = UNITS[u]
        for m in range(first, first + count):
            load_copy(u, m).start()

    def spots(u):
        k, first, count, _ = UNITS[u]
        return k, pl.ds(2 * first, 2 * count)

    def core_copy(u):
        k, part = spots(u)
        return pltpu.make_async_remote_copy(
            src_ref=local.at[k, 1 - core, :, :, part], dst_ref=from_core.at[k, :, :, part],
            send_sem=core_send.at[u], recv_sem=core_recv.at[u],
            device_id=core_peer, device_id_type=MESH)

    def remote(src, dst, send_sem, recv_sem, peer):
        return pltpu.make_async_remote_copy(
            src_ref=src, dst_ref=dst, send_sem=send_sem, recv_sem=recv_sem,
            device_id=peer, device_id_type=MESH)

    def first_copy(u):
        k, part = spots(u)
        if UNITS[u][3] == "P":
            return remote(chip.at[k, 1 - half, :, part], from_pair.at[k, :, part],
                          first_send.at[u], first_recv.at[u], pair_peer)
        return remote(chip.at[k, :, 1 - item, part], from_skip.at[k, :, part],
                      first_send.at[u], first_recv.at[u], cross_peer)

    def second_copy(u):
        k, part = spots(u)
        if UNITS[u][3] == "P":
            return remote(pair.at[k, 1 - item, part], from_cross.at[k, part],
                          second_send.at[u], second_recv.at[u], cross_peer)
        return remote(gap.at[k, part], from_gap.at[k, part],
                      second_send.at[u], second_recv.at[u], pair_peer)

    def third_copy(u):
        k, part = spots(u)
        return remote(merged.at[k, part], from_merged.at[k, part],
                      third_send.at[u], third_recv.at[u], pair_peer)

    def group_copy(k):
        return remote(group.at[k], from_group.at[k], group_send.at[k], group_recv.at[k], tri_peer)

    def plane_copy(k, t, other):
        yy, xx = place_of(other)
        return pltpu.make_async_remote_copy(
            src_ref=quad.at[k, other], dst_ref=gathered.at[k, tri * SPOTS + spot],
            send_sem=plane_send.at[k], recv_sem=plane_recv.at[k],
            device_id=device(t, yy, xx, z, core), device_id_type=MESH)

    def plane_all(k):
        count = 2 * SPOTS - 1 if k in FAR else SPOTS - 1
        return remote(gathered.at[k, pl.ds(0, count)], gathered.at[k, pl.ds(0, count)],
                      plane_send.at[k], plane_recv.at[k], core_peer)

    mask_copy = pltpu.make_async_copy(mask_in, tile_mask, small_sem.at[0])
    depth_copy = pltpu.make_async_copy(depth_in, depth, small_sem.at[1])
    mask_copy.start()
    depth_copy.start()
    for u in LOADS[:2]:
        load_start(u)

    barrier = pltpu.get_barrier_semaphore()
    for peer in (core_peer, pair_peer, cross_peer):
        pl.semaphore_signal(barrier, inc=1, device_id=peer, device_id_type=MESH)
    for step in range(1, 2 * SPOTS):
        t = (tri + step // SPOTS) % 2
        yy, xx = place_of((spot + step) % SPOTS)
        pl.semaphore_signal(barrier, inc=1, device_id=device(t, yy, xx, z, core), device_id_type=MESH)

    for u in LOADS[2:]:
        load_start(u)
    mask_copy.wait()
    depth_copy.wait()

    def nearer(left, right):
        return jnp.where(
            depth[RANK_DEV * left] < depth[RANK_DEV * right], 1.0, 0.0).astype(jnp.float32)

    own = [depth[RANK_DEV * me + r] for r in range(RANK_DEV)]
    front = [[jnp.where(own[j] < own[r], 1.0, 0.0).astype(jnp.float32) for r in range(RANK_DEV)]
             for j in range(RANK_DEV)]

    def number(peer):
        return peer[0] * BLOCKS + peer[1]

    def flags(peer):
        return nearer(me, number(peer)), nearer(number(peer), me)

    core_flags = flags(core_peer)
    pair_flags = flags(pair_peer)
    cross_flags = flags(cross_peer)
    group_flags = flags(tri_peer)

    chips = {"w": me, "v": number(cross_peer), "p": number(pair_peer), "q": number(skew_peer)}
    f = {a + b: nearer(chips[a], chips[b]) for a in chips for b in chips if a != b}
    w_between = f["pw"] * f["wq"] + f["qw"] * f["wp"]
    v_between = f["pv"] * f["vq"] + f["qv"] * f["vp"]
    w_ahead = f["wp"] * f["wq"]
    v_ahead = f["vp"] * f["vq"]

    def quad_device(q):
        return (q // 8) * BLOCKS + (q // 2) % 4 * 16 + q % 2 * 8

    def tree_flags(leaves, base):
        levels = []
        span = 1
        while span < leaves:
            levels.append([
                (nearer(base + quad_device(q), base + quad_device(q + span)),
                 nearer(base + quad_device(q + span), base + quad_device(q)))
                for q in range(0, leaves, 2 * span)])
            span *= 2
        return levels

    far_flags = tree_flags(2 * SPOTS, 0) if FAR else None
    near_flags = tree_flags(SPOTS, tri * BLOCKS)

    sub = lax.broadcasted_iota(jnp.int32, (CHUNK_TILES, 128), 0)

    def mask_of(r, group):
        value = jnp.zeros((CHUNK_TILES, 128), jnp.float32)
        for s in range(CHUNK_TILES):
            on = tile_mask[r, 0, CHUNK_TILES * group + s].astype(jnp.float32)
            value = jnp.where(sub == s, on, value)
        return value

    masks = [[mask_of(r, g) for r in range(RANK_DEV)] for g in range(COLUMN_TILES // CHUNK_TILES)]

    def span_of(u):
        k, first, count, _ = UNITS[u]
        return 2 * first, 2 * (first + count)

    def blend_local(u, to_core):
        k = UNITS[u][0]
        mask = masks[k % (COLUMN_TILES // CHUNK_TILES)]
        first, stop = span_of(u)
        size = stop - first

        @pl.loop(0, 4 * size, unroll=2)
        def _(n):
            hh, ii, o = n // (2 * size), n // size % 2, first + n % size
            block = (hh + ii * (3 - 2 * hh)) * 2 + to_core

            def plane(r, ch):
                return inb[k, o // 2, r, o % 2, block,
                           pl.ds(ch, CHUNK_TILES, stride=CHANNELS), :]

            opacity = [mask[r] * plane(r, 3) for r in range(RANK_DEV)]
            weights = []
            for r in range(RANK_DEV):
                weight = mask[r]
                for j in range(RANK_DEV):
                    if j != r:
                        weight = weight * (1.0 - front[j][r] * opacity[j])
                weights.append(weight)
            for ch in range(CHANNELS):
                total = weights[0] * plane(0, ch)
                for r in range(1, RANK_DEV):
                    total = total + weights[r] * plane(r, ch)
                local[k, to_core, hh, ii, o, ch] = total

    def planes(ref, *index):
        return [ref[index + (ch,)] for ch in range(CHANNELS)]

    def blend_chip(u, sent):
        k, _, _, kind = UNITS[u]
        first, stop = span_of(u)
        size = stop - first

        @pl.loop(0, 2 * size, unroll=2)
        def _(n):
            o = first + n % size
            if kind == "P":
                hh, ii = 1 - half if sent else half, n // size
            else:
                hh, ii = n // size, 1 - item if sent else item
            a = planes(local, k, core, hh, ii, o)
            b = planes(from_core, k, hh, ii, o)
            for ch, value in enumerate(over(a, b, *core_flags)):
                chip[k, hh, ii, o, ch] = value

    def blend_pair(u, to_item):
        k = UNITS[u][0]

        @pl.loop(*span_of(u), unroll=2)
        def _(o):
            a = planes(chip, k, half, to_item, o)
            b = planes(from_pair, k, to_item, o)
            for ch, value in enumerate(over(a, b, *pair_flags)):
                pair[k, to_item, o, ch] = value

    def blend_cross(u):
        k = UNITS[u][0]

        @pl.loop(*span_of(u), unroll=2)
        def _(o):
            a = planes(pair, k, item, o)
            b = planes(from_cross, k, o)
            for ch, value in enumerate(over(a, b, *cross_flags)):
                quad[k, o, ch] = value

    def blend_gap(u):
        k = UNITS[u][0]

        @pl.loop(*span_of(u), unroll=2)
        def _(o):
            gap[k, o] = ((1.0 - w_between * chip[k, half, item, o, 3])
                         * (1.0 - v_between * from_skip[k, half, o, 3]))

    def blend_merged(u):
        k = UNITS[u][0]

        @pl.loop(*span_of(u), unroll=2)
        def _(o):
            w = planes(chip, k, 1 - half, item, o)
            v = planes(from_skip, k, 1 - half, o)
            g = from_gap[k, o]
            weight_w = f["wv"] + f["vw"] * ((1.0 - v[3]) * g)
            weight_v = f["vw"] + f["wv"] * ((1.0 - w[3]) * g)
            for ch in range(3):
                merged[k, o, ch] = weight_w * w[ch] + weight_v * v[ch]
            merged[k, o, 3] = w[3]
            merged[k, o, 4] = v[3]

    def blend_skip(u):
        k = UNITS[u][0]

        @pl.loop(*span_of(u), unroll=2)
        def _(o):
            w = planes(chip, k, half, item, o)
            v = planes(from_skip, k, half, o)
            g = gap[k, o]
            p = from_merged[k, o, 3]
            q = from_merged[k, o, 4]
            m = [from_merged[k, o, ch] for ch in range(3)]
            m.append((f["pq"] + f["qp"] * ((1.0 - q) * g)) * p
                     + (f["qp"] + f["pq"] * ((1.0 - p) * g)) * q)
            weight_w = (1.0 - f["vw"] * v[3]) * (1.0 - f["pw"] * p) * (1.0 - f["qw"] * q)
            weight_v = (1.0 - f["wv"] * w[3]) * (1.0 - f["pv"] * p) * (1.0 - f["qv"] * q)
            weight_m = (1.0 - w_ahead * w[3]) * (1.0 - v_ahead * v[3])
            for ch in range(CHANNELS):
                quad[k, o, ch] = weight_w * w[ch] + weight_v * v[ch] + weight_m * m[ch]

    def blend_tree(k, leaves, base, levels):
        for ch in range(CHANNELS):
            gathered[k, tri * SPOTS + spot, ch] = quad[k, spot, ch]
        images = []
        for q in range(leaves):
            slot = base + (q // SPOTS) * SPOTS + spot_of((q // 2) % 4, q % 2)
            images.append(planes(gathered, k, slot))
        for level in levels:
            images = [over(images[2 * n], images[2 * n + 1], *level[n]) for n in range(len(level))]
        return images[0]

    def put(k, image):
        for ch in range(CHANNELS):
            outv[pl.ds(ROWS * k + ch, CHUNK_TILES, stride=CHANNELS), :] = image[ch]

    def stage_load(u):
        with jax.named_scope(f"L_wait{u}"):
            load_wait(u)
        with jax.named_scope(f"L_send{u}"):
            blend_local(u, 1 - core)
        if u == LOADS[0]:
            with jax.named_scope("w_barrier"):
                pl.semaphore_wait(barrier, 18)
        core_copy(u).start()
        with jax.named_scope(f"L_own{u}"):
            blend_local(u, core)

    def stage_chip(u):
        with jax.named_scope(f"C_wait{u}"):
            core_copy(u).wait_recv()
        with jax.named_scope(f"C_run{u}"):
            blend_chip(u, True)

    def stage_send(u):
        first_copy(u).start()
        with jax.named_scope(f"S_run{u}"):
            blend_chip(u, False)

    def stage_first(u):
        with jax.named_scope(f"A_wait{u}"):
            first_copy(u).wait_recv()
        if UNITS[u][3] == "P":
            with jax.named_scope(f"A_run{u}"):
                blend_pair(u, 1 - item)
            second_copy(u).start()
            blend_pair(u, item)
        else:
            with jax.named_scope(f"A_run{u}"):
                blend_gap(u)
            second_copy(u).start()

    def send_planes(u):
        k, first, count, _ = UNITS[u]
        for step in range(4 * count if k in FAR else 2 * count):
            other = 2 * first + (spot + step) % (2 * count)
            t = (tri + 1 + step // (2 * count)) % 2 if k in FAR else tri

            @pl.when((t != tri) | (other != spot))
            def _():
                plane_copy(k, t, other).start()

    def stage_second(u):
        with jax.named_scope(f"B_wait{u}"):
            second_copy(u).wait_recv()
        if UNITS[u][3] == "P":
            with jax.named_scope(f"B_run{u}"):
                blend_cross(u)
                send_planes(u)
        else:
            with jax.named_scope(f"B_run{u}"):
                blend_merged(u)
            third_copy(u).start()

    def stage_third(u):
        with jax.named_scope(f"D_wait{u}"):
            third_copy(u).wait_recv()
        with jax.named_scope(f"D_run{u}"):
            blend_skip(u)
            send_planes(u)

    def stage_group(k):
        with jax.named_scope(f"G_wait{k}"):
            plane_all(k).wait_recv()
        with jax.named_scope(f"G_run{k}"):
            for ch, value in enumerate(blend_tree(k, SPOTS, tri * SPOTS, near_flags)):
                group[k, ch] = value
        group_copy(k).start()

    def stage_out(k):
        if k in FAR:
            with jax.named_scope(f"F_wait{k}"):
                plane_all(k).wait_recv()
            with jax.named_scope(f"F_run{k}"):
                put(k, blend_tree(k, 2 * SPOTS, 0, far_flags))
        else:
            with jax.named_scope(f"F_wait{k}"):
                group_copy(k).wait_recv()
            with jax.named_scope(f"F_run{k}"):
                put(k, over(planes(group, k), planes(from_group, k), *group_flags))

    stages = {"L": stage_load, "C": stage_chip, "S": stage_send, "A": stage_first,
              "B": stage_second, "D": stage_third, "G": stage_group, "F": stage_out}
    for name, which in PLAN:
        stages[name](which)
    with jax.named_scope("w_sends"):
        for u in range(len(UNITS)):
            core_copy(u).wait_send()
            first_copy(u).wait_send()
            second_copy(u).wait_send()
            if UNITS[u][3] == "T":
                third_copy(u).wait_send()
        for k in range(CHUNKS):
            plane_all(k).wait_send()
            if k not in FAR:
                group_copy(k).wait_send()
    with jax.named_scope("w_out"):
        result = pltpu.make_async_copy(outv, out, small_sem.at[0])
        result.start()
        result.wait()


def on_device(layers, tile_mask, depth_order):
    rank_dev, channels, pixels = layers.shape
    tiles = pixels // 128
    rows = layers.reshape(rank_dev, channels, tiles, 128).transpose(0, 2, 1, 3)
    rows = rows.reshape(rank_dev, 2, 4, 8, BLOCK_TILES * channels, 128)
    plane = (CHUNK_TILES, 128)
    image = (CHANNELS,) + plane
    units = len(UNITS)
    dma = pltpu.SemaphoreType.DMA
    out = pl.pallas_call(
        kernel,
        out_shape=jax.ShapeDtypeStruct((BLOCK_TILES * channels, 128), jnp.float32),
        in_specs=[pl.BlockSpec(memory_space=pltpu.HBM)] * 3,
        out_specs=pl.BlockSpec(memory_space=pl.ANY),
        scratch_shapes=[
            pltpu.VMEM((CHUNKS, 4, rank_dev, 2, 8, ROWS, 128), jnp.float32),
            pltpu.VMEM((CHUNKS, 2, 2, 2, SPOTS) + image, jnp.float32),
            pltpu.VMEM((CHUNKS, 2, 2, SPOTS) + image, jnp.float32),
            pltpu.VMEM((CHUNKS, 2, 2, SPOTS) + image, jnp.float32),
            pltpu.VMEM((CHUNKS, 2, SPOTS) + image, jnp.float32),
            pltpu.VMEM((CHUNKS, 2, SPOTS) + image, jnp.float32),
            pltpu.VMEM((CHUNKS, SPOTS) + image, jnp.float32),
            pltpu.VMEM((CHUNKS, 2, SPOTS) + image, jnp.float32),
            pltpu.VMEM((CHUNKS, SPOTS) + plane, jnp.float32),
            pltpu.VMEM((CHUNKS, SPOTS) + plane, jnp.float32),
            pltpu.VMEM((CHUNKS, SPOTS, 5) + plane, jnp.float32),
            pltpu.VMEM((CHUNKS, SPOTS, 5) + plane, jnp.float32),
            pltpu.VMEM((CHUNKS, SPOTS) + image, jnp.float32),
            pltpu.VMEM((CHUNKS, 2 * SPOTS) + image, jnp.float32),
            pltpu.VMEM((CHUNKS,) + image, jnp.float32),
            pltpu.VMEM((CHUNKS,) + image, jnp.float32),
            pltpu.VMEM((BLOCK_TILES * channels, 128), jnp.float32),
            pltpu.SMEM(tile_mask.shape, jnp.int32),
            pltpu.SMEM(depth_order.shape, jnp.int32),
            dma((units,)),
            dma((units,)), dma((units,)),
            dma((units,)), dma((units,)),
            dma((units,)), dma((units,)),
            dma((units,)), dma((units,)),
            dma((CHUNKS,)), dma((CHUNKS,)),
            dma((CHUNKS,)), dma((CHUNKS,)),
            dma((2,)),
        ],
        compiler_params=pltpu.CompilerParams(
            collective_id=0, has_side_effects=True, vmem_limit_bytes=60 * 1024 * 1024),
    )(rows, tile_mask, depth_order)
    out = out.reshape(BLOCK_TILES, channels, 128).transpose(1, 0, 2)
    return out.reshape(channels, BLOCK_TILES * 128)


def solution(mesh):
    in_specs = (P(("tri", "blk"), None, None), P(("tri", "blk"), None, None), P())
    out_specs = P(None, "blk")
    return jax.shard_map(
        on_device, mesh=mesh, in_specs=in_specs, out_specs=out_specs, check_vma=False
    )
```

time: 56.8 us -> 53.2 us (0.937); the launches traced: 55.7 us -> 53.1 us
  Pallas kernels: 54.2 us -> 51.5 us
    pallas_call x1, Pallas kernels: 54.2 us -> 51.5 us  [on_device(): pl.pallas_call(kernel, out_shape=jax.ShapeDtypeStruct((BLOCK_TILES * chan...]
where the time goes in v3:
time: 53.2 us; the launch traced here: 53.1 us
  Pallas kernels  51.5 us (97%)
  local copies, waits for them, and re-layouts  1.54 us (3%)
    pallas_call x1, Pallas kernels, on_device(): pl.pallas_call(kernel, out_shape=jax.ShapeDtypeStruct((BLOCK_TILES * chan...  51.5 us
    unnamed x1, local copies, waits for them, and re-layouts  1.54 us

profile of v3, /device:TPU:0, one launch (start us, length us, event | category | flops | bytes accessed | tf_op | source)
XLA Modules:
  0.0 53.1 jit_solution(5724133503619566006)
XLA Ops:
  0.0 51.5 %shard_map.37 = f32[192,128]{1,0:T(8,128)} custom-call(f32[3,2,4,8,192,128]{5,4,3,2,1,0:T(8,128)} %bitcast.10, s32[3,1,24]{2,1,0:T(1,128)} %mask_in.1, s32[384]{0:T(512)} %depth_in.1), custom_call_target="tpu_custom_call" | custom-call | tf_op jit(solution)/shard_map/pallas_call | solution.py:479
  51.5 1.5 %copy.7 = f32[4,6144]{1,0:T(4,128)} copy(f32[4,6144]{1,0:T(4,128)} %bitcast.11) | data formatting | bytes 196608

commit v4 on v3

--- a/solution.py
+++ b/solution.py
@@ -17,45 +17,46 @@
 SPOTS = 8
 UNITS = (
     (0, 0, 1, 'P'),
-    (0, 1, 1, 'P'),
-    (0, 2, 1, 'P'),
+    (0, 1, 2, 'P'),
     (0, 3, 1, 'P'),
-    (1, 0, 4, 'P'),
+    (1, 0, 1, 'P'),
+    (1, 1, 2, 'P'),
+    (1, 3, 1, 'P'),
     (2, 0, 2, 'P'),
-    (2, 2, 1, 'T'),
-    (2, 3, 1, 'T'),
-    (3, 0, 2, 'T'),
-    (3, 2, 2, 'T'),
+    (2, 2, 2, 'T'),
+    (3, 0, 1, 'T'),
+    (3, 1, 2, 'T'),
+    (3, 3, 1, 'T'),
     (4, 0, 4, 'T'),
     (5, 0, 1, 'T'),
     (5, 1, 1, 'T'),
     (5, 2, 1, 'T'),
     (5, 3, 1, 'T'),
 )
-LOADS = (3, 6, 1, 10, 2, 4, 5, 9, 8, 0, 14, 7, 11, 13, 12)
+LOADS = (0, 14, 7, 2, 11, 9, 8, 10, 1, 12, 4, 5, 13, 3, 15, 6)
 FAR = (5,)
 PLAN = (
-    ('L', 3), ('L', 6), ('L', 1), ('L', 10), ('C', 3), ('S', 3), ('C', 6), ('S', 6), ('C', 1),
-    ('S', 1), ('L', 2), ('L', 4), ('C', 10), ('S', 10), ('C', 2), ('S', 2), ('L', 5), ('L', 9),
-    ('L', 8), ('A', 3), ('A', 6), ('C', 4), ('S', 4), ('C', 5), ('L', 0), ('L', 14), ('C', 9),
-    ('L', 7), ('L', 11), ('C', 8), ('A', 1), ('L', 13), ('C', 0), ('L', 12), ('C', 14), ('C', 7),
-    ('S', 9), ('C', 11), ('C', 13), ('A', 2), ('C', 12), ('B', 6), ('A', 10), ('S', 8), ('B', 3),
-    ('B', 1), ('S', 5), ('S', 14), ('A', 4), ('D', 6), ('A', 9), ('B', 10), ('B', 2), ('S', 7),
-    ('A', 5), ('B', 9), ('A', 8), ('A', 14), ('S', 11), ('S', 0), ('D', 10), ('S', 13), ('B', 4),
-    ('S', 12), ('D', 9), ('B', 8), ('A', 7), ('B', 14), ('B', 5), ('A', 0), ('A', 11), ('G', 4),
-    ('D', 8), ('B', 7), ('A', 13), ('D', 14), ('B', 11), ('G', 1), ('A', 12), ('D', 7), ('B', 13),
-    ('B', 0), ('F', 4), ('D', 11), ('B', 12), ('G', 3), ('D', 13), ('F', 1), ('D', 12), ('G', 2),
-    ('G', 0), ('F', 3), ('F', 2), ('F', 0), ('F', 5),
+    ('L', 0), ('L', 14), ('L', 7), ('L', 2), ('L', 11), ('C', 0), ('S', 0), ('C', 14), ('S', 14),
+    ('L', 9), ('C', 7), ('S', 7), ('C', 2), ('S', 2), ('L', 8), ('L', 10), ('L', 1), ('C', 11),
+    ('S', 11), ('C', 9), ('L', 12), ('C', 8), ('L', 4), ('C', 10), ('L', 5), ('C', 1), ('S', 1),
+    ('S', 9), ('A', 0), ('A', 14), ('L', 13), ('C', 12), ('L', 3), ('L', 15), ('L', 6), ('C', 4),
+    ('S', 4), ('C', 5), ('C', 13), ('A', 2), ('C', 3), ('S', 5), ('C', 15), ('C', 6), ('A', 7),
+    ('S', 3), ('S', 8), ('A', 1), ('B', 14), ('S', 6), ('S', 10), ('A', 4), ('A', 11), ('A', 5),
+    ('B', 7), ('S', 12), ('A', 3), ('A', 9), ('D', 14), ('B', 0), ('S', 13), ('B', 2), ('S', 15),
+    ('A', 8), ('A', 6), ('B', 11), ('B', 1), ('D', 7), ('A', 10), ('B', 9), ('B', 8), ('B', 4),
+    ('B', 5), ('A', 12), ('D', 11), ('B', 10), ('G', 0), ('B', 3), ('A', 13), ('D', 9), ('D', 8),
+    ('B', 12), ('A', 15), ('D', 10), ('B', 13), ('B', 6), ('D', 12), ('B', 15), ('D', 13), ('G', 4),
+    ('G', 1), ('D', 15), ('G', 3), ('G', 2), ('F', 0), ('F', 4), ('F', 1), ('F', 3), ('F', 5),
+    ('F', 2),
 )
 
 
 def spot_of(y, x):
-    return 4 * ((y + x) % 2) + 2 * x + y // 2
+    return 2 * y + x
 
 
 def place_of(spot):
-    x = (spot // 2) % 2
-    return 2 * (spot % 2) + (x + spot // 4) % 2, x
+    return spot // 2, spot % 2
 
 
 def over(a, b, a_front, b_front):
@@ -67,8 +68,8 @@
 def kernel(layers, mask_in, depth_in, out,
            inb, local, from_core, chip, from_pair, pair, from_cross, from_skip, gap, from_gap,
            merged, from_merged, quad, gathered, group, from_group, outv, tile_mask, depth,
-           in_sem, core_send, core_recv, first_send, first_recv, second_send, second_recv,
-           third_send, third_recv, plane_send, plane_recv, group_send, group_recv, small_sem):
+           in_sem, core_recv, first_recv, second_recv, third_recv, plane_recv, group_recv, sent,
+           small_sem):
     tri = lax.axis_index("tri")
     blk = lax.axis_index("blk")
     core = blk % 2
@@ -91,9 +92,8 @@
 
     def load_copy(u, m):
         k, first, _, _ = UNITS[u]
-        low = (m % 2 + m // 2) % 2 * 2 + m % 2
         return pltpu.make_async_copy(
-            layers.at[:, :, low, :, pl.ds(ROWS * k, ROWS), :], inb.at[k, m], in_sem.at[u])
+            layers.at[:, m, :, :, pl.ds(ROWS * k, ROWS), :], inb.at[k, m], in_sem.at[u])
 
     def load_wait(u):
         k, first, count, _ = UNITS[u]
@@ -113,7 +113,7 @@
         k, part = spots(u)
         return pltpu.make_async_remote_copy(
             src_ref=local.at[k, 1 - core, :, :, part], dst_ref=from_core.at[k, :, :, part],
-            send_sem=core_send.at[u], recv_sem=core_recv.at[u],
+            send_sem=sent.at[0], recv_sem=core_recv.at[u],
             device_id=core_peer, device_id_type=MESH)
 
     def remote(src, dst, send_sem, recv_sem, peer):
@@ -125,37 +125,51 @@
         k, part = spots(u)
         if UNITS[u][3] == "P":
             return remote(chip.at[k, 1 - half, :, part], from_pair.at[k, :, part],
-                          first_send.at[u], first_recv.at[u], pair_peer)
+                          sent.at[1], first_recv.at[u], pair_peer)
         return remote(chip.at[k, :, 1 - item, part], from_skip.at[k, :, part],
-                      first_send.at[u], first_recv.at[u], cross_peer)
+                      sent.at[1], first_recv.at[u], cross_peer)
+
+    def flat(u):
+        k, first, count, _ = UNITS[u]
+        return pl.ds(SPOTS * k + 2 * first, 2 * count)
 
     def second_copy(u):
         k, part = spots(u)
         if UNITS[u][3] == "P":
-            return remote(pair.at[k, 1 - item, part], from_cross.at[k, part],
-                          second_send.at[u], second_recv.at[u], cross_peer)
-        return remote(gap.at[k, part], from_gap.at[k, part],
-                      second_send.at[u], second_recv.at[u], pair_peer)
+            return remote(pair.at[k, 1 - item, part], from_cross.at[flat(u)],
+                          sent.at[2], second_recv.at[u], cross_peer)
+        return remote(gap.at[flat(u)], from_gap.at[flat(u)],
+                      sent.at[3], second_recv.at[u], pair_peer)
 
     def third_copy(u):
-        k, part = spots(u)
-        return remote(merged.at[k, part], from_merged.at[k, part],
-                      third_send.at[u], third_recv.at[u], pair_peer)
+        return remote(merged.at[flat(u)], from_merged.at[flat(u)],
+                      sent.at[4], third_recv.at[u], pair_peer)
 
     def group_copy(k):
-        return remote(group.at[k], from_group.at[k], group_send.at[k], group_recv.at[k], tri_peer)
+        return remote(group.at[k], from_group.at[k], sent.at[5], group_recv.at[k], tri_peer)
+
+    def all_sent():
+        plain = sum(2 * unit[2] for unit in UNITS if unit[3] == "P")
+        skip = sum(2 * unit[2] for unit in UNITS if unit[3] == "T")
+        near = CHUNKS - len(FAR)
+        plane_copies = near * (SPOTS - 1) + len(FAR) * (2 * SPOTS - 1)
+        for n, ref in enumerate((
+                from_core, from_skip, from_cross.at[pl.ds(0, plain)], from_gap.at[pl.ds(0, skip)],
+                from_merged.at[pl.ds(0, skip)], group.at[pl.ds(0, near)],
+                gathered.at[pl.ds(0, plane_copies)])):
+            remote(ref, ref, sent.at[n], core_recv.at[0], core_peer).wait_send()
 
     def plane_copy(k, t, other):
         yy, xx = place_of(other)
         return pltpu.make_async_remote_copy(
-            src_ref=quad.at[k, other], dst_ref=gathered.at[k, tri * SPOTS + spot],
-            send_sem=plane_send.at[k], recv_sem=plane_recv.at[k],
+            src_ref=quad.at[k, other], dst_ref=gathered.at[2 * SPOTS * k + tri * SPOTS + spot],
+            send_sem=sent.at[6], recv_sem=plane_recv.at[k],
             device_id=device(t, yy, xx, z, core), device_id_type=MESH)
 
     def plane_all(k):
         count = 2 * SPOTS - 1 if k in FAR else SPOTS - 1
-        return remote(gathered.at[k, pl.ds(0, count)], gathered.at[k, pl.ds(0, count)],
-                      plane_send.at[k], plane_recv.at[k], core_peer)
+        return remote(gathered.at[pl.ds(0, count)], gathered.at[pl.ds(0, count)],
+                      sent.at[6], plane_recv.at[k], core_peer)
 
     mask_copy = pltpu.make_async_copy(mask_in, tile_mask, small_sem.at[0])
     depth_copy = pltpu.make_async_copy(depth_in, depth, small_sem.at[1])
@@ -238,51 +252,46 @@
     def blend_local(u, to_core):
         k = UNITS[u][0]
         mask = masks[k % (COLUMN_TILES // CHUNK_TILES)]
-        first, stop = span_of(u)
-        size = stop - first
-
-        @pl.loop(0, 4 * size, unroll=2)
-        def _(n):
-            hh, ii, o = n // (2 * size), n // size % 2, first + n % size
-            block = (hh + ii * (3 - 2 * hh)) * 2 + to_core
-
-            def plane(r, ch):
-                return inb[k, o // 2, r, o % 2, block,
-                           pl.ds(ch, CHUNK_TILES, stride=CHANNELS), :]
-
-            opacity = [mask[r] * plane(r, 3) for r in range(RANK_DEV)]
-            weights = []
-            for r in range(RANK_DEV):
-                weight = mask[r]
-                for j in range(RANK_DEV):
-                    if j != r:
-                        weight = weight * (1.0 - front[j][r] * opacity[j])
-                weights.append(weight)
-            for ch in range(CHANNELS):
-                total = weights[0] * plane(0, ch)
-                for r in range(1, RANK_DEV):
-                    total = total + weights[r] * plane(r, ch)
-                local[k, to_core, hh, ii, o, ch] = total
+        @pl.loop(*span_of(u))
+        def _(o):
+            for hh, ii in ((0, 0), (0, 1), (1, 0), (1, 1)):
+                block = (hh + ii * (3 - 2 * hh)) * 2 + to_core
+
+                def plane(r, ch):
+                    return inb[k, o // 2, r, o % 2, block,
+                               pl.ds(ch, CHUNK_TILES, stride=CHANNELS), :]
+
+                opacity = [mask[r] * plane(r, 3) for r in range(RANK_DEV)]
+                weights = []
+                for r in range(RANK_DEV):
+                    weight = mask[r]
+                    for j in range(RANK_DEV):
+                        if j != r:
+                            weight = weight * (1.0 - front[j][r] * opacity[j])
+                    weights.append(weight)
+                for ch in range(CHANNELS):
+                    total = weights[0] * plane(0, ch)
+                    for r in range(1, RANK_DEV):
+                        total = total + weights[r] * plane(r, ch)
+                    local[k, to_core, hh, ii, o, ch] = total
 
     def planes(ref, *index):
         return [ref[index + (ch,)] for ch in range(CHANNELS)]
 
     def blend_chip(u, sent):
         k, _, _, kind = UNITS[u]
-        first, stop = span_of(u)
-        size = stop - first
-
-        @pl.loop(0, 2 * size, unroll=2)
-        def _(n):
-            o = first + n % size
-            if kind == "P":
-                hh, ii = 1 - half if sent else half, n // size
-            else:
-                hh, ii = n // size, 1 - item if sent else item
-            a = planes(local, k, core, hh, ii, o)
-            b = planes(from_core, k, hh, ii, o)
-            for ch, value in enumerate(over(a, b, *core_flags)):
-                chip[k, hh, ii, o, ch] = value
+
+        @pl.loop(*span_of(u))
+        def _(o):
+            for n in range(2):
+                if kind == "P":
+                    hh, ii = 1 - half if sent else half, n
+                else:
+                    hh, ii = n, 1 - item if sent else item
+                a = planes(local, k, core, hh, ii, o)
+                b = planes(from_core, k, hh, ii, o)
+                for ch, value in enumerate(over(a, b, *core_flags)):
+                    chip[k, hh, ii, o, ch] = value
 
     def blend_pair(u, to_item):
         k = UNITS[u][0]
@@ -300,7 +309,7 @@
         @pl.loop(*span_of(u), unroll=2)
         def _(o):
             a = planes(pair, k, item, o)
-            b = planes(from_cross, k, o)
+            b = planes(from_cross, SPOTS * k + o)
             for ch, value in enumerate(over(a, b, *cross_flags)):
                 quad[k, o, ch] = value
 
@@ -309,7 +318,7 @@
 
         @pl.loop(*span_of(u), unroll=2)
         def _(o):
-            gap[k, o] = ((1.0 - w_between * chip[k, half, item, o, 3])
+            gap[SPOTS * k + o] = ((1.0 - w_between * chip[k, half, item, o, 3])
                          * (1.0 - v_between * from_skip[k, half, o, 3]))
 
     def blend_merged(u):
@@ -319,13 +328,13 @@
         def _(o):
             w = planes(chip, k, 1 - half, item, o)
             v = planes(from_skip, k, 1 - half, o)
-            g = from_gap[k, o]
+            g = from_gap[SPOTS * k + o]
             weight_w = f["wv"] + f["vw"] * ((1.0 - v[3]) * g)
             weight_v = f["vw"] + f["wv"] * ((1.0 - w[3]) * g)
             for ch in range(3):
-                merged[k, o, ch] = weight_w * w[ch] + weight_v * v[ch]
-            merged[k, o, 3] = w[3]
-            merged[k, o, 4] = v[3]
+                merged[SPOTS * k + o, ch] = weight_w * w[ch] + weight_v * v[ch]
+            merged[SPOTS * k + o, 3] = w[3]
+            merged[SPOTS * k + o, 4] = v[3]
 
     def blend_skip(u):
         k = UNITS[u][0]
@@ -334,10 +343,10 @@
         def _(o):
             w = planes(chip, k, half, item, o)
             v = planes(from_skip, k, half, o)
-            g = gap[k, o]
-            p = from_merged[k, o, 3]
-            q = from_merged[k, o, 4]
-            m = [from_merged[k, o, ch] for ch in range(3)]
+            g = gap[SPOTS * k + o]
+            p = from_merged[SPOTS * k + o, 3]
+            q = from_merged[SPOTS * k + o, 4]
+            m = [from_merged[SPOTS * k + o, ch] for ch in range(3)]
             m.append((f["pq"] + f["qp"] * ((1.0 - q) * g)) * p
                      + (f["qp"] + f["pq"] * ((1.0 - p) * g)) * q)
             weight_w = (1.0 - f["vw"] * v[3]) * (1.0 - f["pw"] * p) * (1.0 - f["qw"] * q)
@@ -348,11 +357,11 @@
 
     def blend_tree(k, leaves, base, levels):
         for ch in range(CHANNELS):
-            gathered[k, tri * SPOTS + spot, ch] = quad[k, spot, ch]
+            gathered[2 * SPOTS * k + tri * SPOTS + spot, ch] = quad[k, spot, ch]
         images = []
         for q in range(leaves):
-            slot = base + (q // SPOTS) * SPOTS + spot_of((q // 2) % 4, q % 2)
-            images.append(planes(gathered, k, slot))
+            slot = 2 * SPOTS * k + base + (q // SPOTS) * SPOTS + spot_of((q // 2) % 4, q % 2)
+            images.append(planes(gathered, slot))
         for level in levels:
             images = [over(images[2 * n], images[2 * n + 1], *level[n]) for n in range(len(level))]
         return images[0]
@@ -451,16 +460,7 @@
     for name, which in PLAN:
         stages[name](which)
     with jax.named_scope("w_sends"):
-        for u in range(len(UNITS)):
-            core_copy(u).wait_send()
-            first_copy(u).wait_send()
-            second_copy(u).wait_send()
-            if UNITS[u][3] == "T":
-                third_copy(u).wait_send()
-        for k in range(CHUNKS):
-            plane_all(k).wait_send()
-            if k not in FAR:
-                group_copy(k).wait_send()
+        all_sent()
     with jax.named_scope("w_out"):
         result = pltpu.make_async_copy(outv, out, small_sem.at[0])
         result.start()
@@ -471,7 +471,7 @@
     rank_dev, channels, pixels = layers.shape
     tiles = pixels // 128
     rows = layers.reshape(rank_dev, channels, tiles, 128).transpose(0, 2, 1, 3)
-    rows = rows.reshape(rank_dev, 2, 4, 8, BLOCK_TILES * channels, 128)
+    rows = rows.reshape(rank_dev, 4, 2, 8, BLOCK_TILES * channels, 128)
     plane = (CHUNK_TILES, 128)
     image = (CHANNELS,) + plane
     units = len(UNITS)
@@ -488,26 +488,21 @@
             pltpu.VMEM((CHUNKS, 2, 2, SPOTS) + image, jnp.float32),
             pltpu.VMEM((CHUNKS, 2, SPOTS) + image, jnp.float32),
             pltpu.VMEM((CHUNKS, 2, SPOTS) + image, jnp.float32),
+            pltpu.VMEM((CHUNKS * SPOTS,) + image, jnp.float32),
+            pltpu.VMEM((CHUNKS, 2, SPOTS) + image, jnp.float32),
+            pltpu.VMEM((CHUNKS * SPOTS,) + plane, jnp.float32),
+            pltpu.VMEM((CHUNKS * SPOTS,) + plane, jnp.float32),
+            pltpu.VMEM((CHUNKS * SPOTS, 5) + plane, jnp.float32),
+            pltpu.VMEM((CHUNKS * SPOTS, 5) + plane, jnp.float32),
             pltpu.VMEM((CHUNKS, SPOTS) + image, jnp.float32),
-            pltpu.VMEM((CHUNKS, 2, SPOTS) + image, jnp.float32),
-            pltpu.VMEM((CHUNKS, SPOTS) + plane, jnp.float32),
-            pltpu.VMEM((CHUNKS, SPOTS) + plane, jnp.float32),
-            pltpu.VMEM((CHUNKS, SPOTS, 5) + plane, jnp.float32),
-            pltpu.VMEM((CHUNKS, SPOTS, 5) + plane, jnp.float32),
-            pltpu.VMEM((CHUNKS, SPOTS) + image, jnp.float32),
-            pltpu.VMEM((CHUNKS, 2 * SPOTS) + image, jnp.float32),
+            pltpu.VMEM((CHUNKS * 2 * SPOTS,) + image, jnp.float32),
             pltpu.VMEM((CHUNKS,) + image, jnp.float32),
             pltpu.VMEM((CHUNKS,) + image, jnp.float32),
             pltpu.VMEM((BLOCK_TILES * channels, 128), jnp.float32),
             pltpu.SMEM(tile_mask.shape, jnp.int32),
             pltpu.SMEM(depth_order.shape, jnp.int32),
-            dma((units,)),
-            dma((units,)), dma((units,)),
-            dma((units,)), dma((units,)),
-            dma((units,)), dma((units,)),
-            dma((units,)), dma((units,)),
-            dma((CHUNKS,)), dma((CHUNKS,)),
-            dma((CHUNKS,)), dma((CHUNKS,)),
+            dma((units,)), dma((units,)), dma((units,)), dma((units,)), dma((units,)),
+            dma((CHUNKS,)), dma((CHUNKS,)), dma((7,)),
             dma((2,)),
         ],
         compiler_params=pltpu.CompilerParams(

time: 53.2 us -> 50.2 us (0.944)
  Pallas kernels: 51.5 us -> 48.5 us
    pallas_call x1, Pallas kernels: 51.5 us -> 48.5 us  [on_device(): pl.pallas_call(kernel, out_shape=jax.ShapeDtypeStruct((BLOCK_TILES * chan...]
where the time goes in v4:
time: 50.2 us; the launch traced here: 50.1 us
  Pallas kernels  48.5 us (97%)
  local copies, waits for them, and re-layouts  1.54 us (3%)
    pallas_call x1, Pallas kernels, on_device(): pl.pallas_call(kernel, out_shape=jax.ShapeDtypeStruct((BLOCK_TILES * chan...  48.5 us
    unnamed x1, local copies, waits for them, and re-layouts  1.54 us

profile of v4, /device:TPU:0, one launch (start us, length us, event | category | flops | bytes accessed | tf_op | source)
XLA Modules:
  0.0 50.1 jit_solution(5891186666625175233)
XLA Ops:
  0.0 48.5 %shard_map.37 = f32[192,128]{1,0:T(8,128)} custom-call(f32[3,4,2,8,192,128]{5,4,3,2,1,0:T(8,128)} %bitcast.10, s32[3,1,24]{2,1,0:T(1,128)} %mask_in.1, s32[384]{0:T(512)} %depth_in.1), custom_call_target="tpu_custom_call" | custom-call | tf_op jit(solution)/shard_map/pallas_call | solution.py:479
  48.5 1.5 %copy.7 = f32[4,6144]{1,0:T(4,128)} copy(f32[4,6144]{1,0:T(4,128)} %bitcast.11) | data formatting | bytes 196608

commit v5 on v4

--- a/solution.py
+++ b/solution.py
@@ -17,37 +17,40 @@
 SPOTS = 8
 UNITS = (
     (0, 0, 1, 'P'),
-    (0, 1, 2, 'P'),
+    (0, 1, 1, 'P'),
+    (0, 2, 1, 'P'),
     (0, 3, 1, 'P'),
-    (1, 0, 1, 'P'),
-    (1, 1, 2, 'P'),
-    (1, 3, 1, 'P'),
-    (2, 0, 2, 'P'),
-    (2, 2, 2, 'T'),
-    (3, 0, 1, 'T'),
-    (3, 1, 2, 'T'),
+    (1, 0, 4, 'P'),
+    (2, 0, 1, 'P'),
+    (2, 1, 1, 'P'),
+    (2, 2, 1, 'T'),
+    (2, 3, 1, 'T'),
+    (3, 0, 2, 'T'),
+    (3, 2, 1, 'T'),
     (3, 3, 1, 'T'),
-    (4, 0, 4, 'T'),
+    (4, 0, 2, 'T'),
+    (4, 2, 2, 'T'),
     (5, 0, 1, 'T'),
     (5, 1, 1, 'T'),
     (5, 2, 1, 'T'),
     (5, 3, 1, 'T'),
 )
-LOADS = (0, 14, 7, 2, 11, 9, 8, 10, 1, 12, 4, 5, 13, 3, 15, 6)
-FAR = (5,)
+LOADS = (7, 1, 8, 4, 12, 2, 5, 9, 6, 14, 0, 13, 11, 3, 10, 16, 15, 17)
+FAR = (2, 4, 5)
 PLAN = (
-    ('L', 0), ('L', 14), ('L', 7), ('L', 2), ('L', 11), ('C', 0), ('S', 0), ('C', 14), ('S', 14),
-    ('L', 9), ('C', 7), ('S', 7), ('C', 2), ('S', 2), ('L', 8), ('L', 10), ('L', 1), ('C', 11),
-    ('S', 11), ('C', 9), ('L', 12), ('C', 8), ('L', 4), ('C', 10), ('L', 5), ('C', 1), ('S', 1),
-    ('S', 9), ('A', 0), ('A', 14), ('L', 13), ('C', 12), ('L', 3), ('L', 15), ('L', 6), ('C', 4),
-    ('S', 4), ('C', 5), ('C', 13), ('A', 2), ('C', 3), ('S', 5), ('C', 15), ('C', 6), ('A', 7),
-    ('S', 3), ('S', 8), ('A', 1), ('B', 14), ('S', 6), ('S', 10), ('A', 4), ('A', 11), ('A', 5),
-    ('B', 7), ('S', 12), ('A', 3), ('A', 9), ('D', 14), ('B', 0), ('S', 13), ('B', 2), ('S', 15),
-    ('A', 8), ('A', 6), ('B', 11), ('B', 1), ('D', 7), ('A', 10), ('B', 9), ('B', 8), ('B', 4),
-    ('B', 5), ('A', 12), ('D', 11), ('B', 10), ('G', 0), ('B', 3), ('A', 13), ('D', 9), ('D', 8),
-    ('B', 12), ('A', 15), ('D', 10), ('B', 13), ('B', 6), ('D', 12), ('B', 15), ('D', 13), ('G', 4),
-    ('G', 1), ('D', 15), ('G', 3), ('G', 2), ('F', 0), ('F', 4), ('F', 1), ('F', 3), ('F', 5),
-    ('F', 2),
+    ('L', 7), ('L', 1), ('L', 8), ('L', 4), ('C', 7), ('S', 7), ('L', 12), ('C', 1), ('S', 1),
+    ('C', 8), ('S', 8), ('L', 2), ('L', 5), ('L', 9), ('C', 4), ('L', 6), ('S', 4), ('C', 12),
+    ('S', 12), ('C', 2), ('C', 5), ('L', 14), ('L', 0), ('L', 13), ('C', 9), ('S', 9), ('C', 6),
+    ('L', 11), ('A', 7), ('L', 3), ('C', 14), ('L', 10), ('A', 1), ('C', 0), ('L', 16), ('L', 15),
+    ('C', 13), ('L', 17), ('C', 11), ('A', 8), ('C', 3), ('C', 10), ('C', 16), ('C', 15), ('C', 17),
+    ('S', 14), ('A', 12), ('S', 13), ('S', 2), ('A', 4), ('B', 7), ('B', 8), ('B', 12), ('A', 9),
+    ('B', 1), ('A', 2), ('D', 7), ('A', 14), ('D', 8), ('S', 5), ('S', 11), ('D', 12), ('S', 6),
+    ('A', 13), ('B', 9), ('S', 10), ('B', 14), ('S', 16), ('A', 5), ('B', 4), ('A', 6), ('B', 13),
+    ('B', 2), ('S', 15), ('A', 11), ('D', 9), ('S', 17), ('D', 14), ('S', 0), ('A', 10), ('S', 3),
+    ('A', 16), ('D', 13), ('B', 11), ('B', 5), ('B', 6), ('A', 0), ('G', 1), ('B', 10), ('A', 15),
+    ('A', 3), ('B', 16), ('A', 17), ('D', 11), ('B', 0), ('D', 10), ('B', 15), ('B', 3), ('D', 16),
+    ('B', 17), ('D', 15), ('G', 3), ('D', 17), ('G', 0), ('F', 1), ('F', 4), ('F', 2), ('F', 3),
+    ('F', 5), ('F', 0),
 )
 
 
@@ -67,7 +70,7 @@
 
 def kernel(layers, mask_in, depth_in, out,
            inb, local, from_core, chip, from_pair, pair, from_cross, from_skip, gap, from_gap,
-           merged, from_merged, quad, gathered, group, from_group, outv, tile_mask, depth,
+           merged, from_merged, quad, gathered, group, from_group, tile_mask, depth,
            in_sem, core_recv, first_recv, second_recv, third_recv, plane_recv, group_recv, sent,
            small_sem):
     tri = lax.axis_index("tri")
@@ -368,7 +371,7 @@
 
     def put(k, image):
         for ch in range(CHANNELS):
-            outv[pl.ds(ROWS * k + ch, CHUNK_TILES, stride=CHANNELS), :] = image[ch]
+            out[pl.ds(ROWS * k + ch, CHUNK_TILES, stride=CHANNELS), :] = image[ch]
 
     def stage_load(u):
         with jax.named_scope(f"L_wait{u}"):
@@ -461,10 +464,6 @@
         stages[name](which)
     with jax.named_scope("w_sends"):
         all_sent()
-    with jax.named_scope("w_out"):
-        result = pltpu.make_async_copy(outv, out, small_sem.at[0])
-        result.start()
-        result.wait()
 
 
 def on_device(layers, tile_mask, depth_order):
@@ -480,7 +479,7 @@
         kernel,
         out_shape=jax.ShapeDtypeStruct((BLOCK_TILES * channels, 128), jnp.float32),
         in_specs=[pl.BlockSpec(memory_space=pltpu.HBM)] * 3,
-        out_specs=pl.BlockSpec(memory_space=pl.ANY),
+        out_specs=pl.BlockSpec(memory_space=pltpu.VMEM),
         scratch_shapes=[
             pltpu.VMEM((CHUNKS, 4, rank_dev, 2, 8, ROWS, 128), jnp.float32),
             pltpu.VMEM((CHUNKS, 2, 2, 2, SPOTS) + image, jnp.float32),
@@ -498,7 +497,6 @@
             pltpu.VMEM((CHUNKS * 2 * SPOTS,) + image, jnp.float32),
             pltpu.VMEM((CHUNKS,) + image, jnp.float32),
             pltpu.VMEM((CHUNKS,) + image, jnp.float32),
-            pltpu.VMEM((BLOCK_TILES * channels, 128), jnp.float32),
             pltpu.SMEM(tile_mask.shape, jnp.int32),
             pltpu.SMEM(depth_order.shape, jnp.int32),
             dma((units,)), dma((units,)), dma((units,)), dma((units,)), dma((units,)),
@@ -506,7 +504,7 @@
             dma((2,)),
         ],
         compiler_params=pltpu.CompilerParams(
-            collective_id=0, has_side_effects=True, vmem_limit_bytes=60 * 1024 * 1024),
+            collective_id=0, has_side_effects=True, vmem_limit_bytes=45 * 1024 * 1024),
     )(rows, tile_mask, depth_order)
     out = out.reshape(BLOCK_TILES, channels, 128).transpose(1, 0, 2)
     return out.reshape(channels, BLOCK_TILES * 128)

time: 50.2 us -> 49.8 us (level)
  Pallas kernels: 48.5 us -> 47.6 us
    pallas_call x1, Pallas kernels: 48.5 us -> 47.6 us  [on_device(): pl.pallas_call(kernel, out_shape=jax.ShapeDtypeStruct((BLOCK_TILES * chan...]
    unnamed x1 -> x5, local copies, waits for them, and re-layouts: 1.54 us -> 2 us
where the time goes in v5:
time: 49.8 us; the launch traced here: 49.6 us
  Pallas kernels  47.6 us (96%)
  local copies, waits for them, and re-layouts  2 us (4%)
    pallas_call x1, Pallas kernels, on_device(): pl.pallas_call(kernel, out_shape=jax.ShapeDtypeStruct((BLOCK_TILES * chan...  47.6 us
    unnamed x5, local copies, waits for them, and re-layouts  2 us

profile of v5, /device:TPU:0, one launch (start us, length us, event | category | flops | bytes accessed | tf_op | source)
XLA Modules:
  0.0 49.6 jit_solution(787394253879098131)
XLA Ops:
  0.0 0.0 copy-start
  0.0 0.7 %copy-done = s32[384]{0:T(512)S(1)} copy-done((s32[384]{0:T(512)S(1)}, s32[384]{0:T(512)}, u32[]{:S(2)}) %copy-start) | copy-done | bytes 1560
  0.7 0.0 copy-start.1
  0.7 0.7 %copy-done.1 = s32[3,1,24]{2,1,0:T(1,128)S(1)} copy-done((s32[3,1,24]{2,1,0:T(1,128)S(1)}, s32[3,1,24]{2,1,0:T(1,128)}, u32[]{:S(2)}) %copy-start.1) | copy-done | bytes 312
  1.4 47.6 %shard_map.37 = f32[192,128]{1,0:T(8,128)S(1)} custom-call(f32[3,4,2,8,192,128]{5,4,3,2,1,0:T(8,128)} %bitcast.11, s32[3,1,24]{2,1,0:T(1,128)S(1)} %copy-done.1, s32[384]{0:T(512)S(1)} %copy-done), custom_call_target="tpu_custom_call" | custom-call | tf_op jit(solution)/shard_map/pallas_call | solution.py:478
  49.0 0.6 %copy.7 = f32[4,6144]{1,0:T(4,128)} copy(f32[4,6144]{1,0:T(4,128)S(1)} %bitcast.10) | data formatting | bytes 196608
Async XLA Ops:
  0.0 0.7 %copy-start = (s32[384]{0:T(512)S(1)}, s32[384]{0:T(512)}, u32[]{:S(2)}) copy-start(s32[384]{0:T(512)} %depth_in.1) | copy-start | bytes 4612
  0.7 0.7 %copy-start.1 = (s32[3,1,24]{2,1,0:T(1,128)S(1)}, s32[3,1,24]{2,1,0:T(1,128)}, u32[]{:S(2)}) copy-start(s32[3,1,24]{2,1,0:T(1,128)} %mask_in.1) | copy-start | bytes 868
